TPU v7x, 32 devices: a whole 2x2x4 slice. The times are simulated.
32 devices in a mesh: gx: 2 (over x), gy: 4 (over y, core), gz: 4 (over z).
Axes of the slice: x: 2, y: 2, z: 4, core: 2. Of those that a mesh axis runs over, the one named last changes fastest.
Arguments:
- right_side: float32 [24, 64, 512], P('gx', 'gy', 'gz'), may hold values from -8 to 8
- coefficient: float32 [24, 64, 512], P('gx', 'gy', 'gz'), may hold values from 0.02 to 1
Outputs:
- solution: float32 [24, 64, 512], P('gx', 'gy', 'gz')
- residual: float32 [24, 64, 512], P('gx', 'gy', 'gz')
- precond: float32 [24, 64, 512], P('gx', 'gy', 'gz')
- image: float32 [24, 64, 512], P('gx', 'gy', 'gz')
All inputs are finite; a program needn't handle non-finite values.
Results may differ from a plain program's by a relative error of at most 0.00021.
Values sent between devices are 32-bit elements; how exact they have to be, the bound alone decides.
A program may use at most 64 MiB of HBM per device.

v0:
```python
import functools

import jax
import jax.numpy as jnp
from jax import lax
from jax.experimental import pallas as pl
from jax.experimental.pallas import tpu as pltpu
from jax.sharding import PartitionSpec as P

SWEEPS = 4
relaxation = 0.6

AXES = ("gx", "gy", "gz")
MESH = pl.DeviceIdType.MESH
WIDTH = 5
EDGE = 8
SPAN = 2 * WIDTH
PART = SWEEPS


def dot(a, b):
    high = a.astype(jnp.bfloat16)
    low = (a - high.astype(jnp.float32)).astype(jnp.bfloat16)
    both = jnp.concatenate([high, low], 1)
    b = b.astype(jnp.bfloat16)
    return jnp.dot(both, jnp.concatenate([b, b], 0), preferred_element_type=jnp.float32)


def iota(shape, dim):
    return lax.broadcasted_iota(jnp.int32, shape, dim)


def kernel(counts, block, reach, g_ref, c_ref, pre_ref, img_ref, twice_ref, image_twice_ref, alpha_ref,
           gc0, im0, pk1, pk2, zr1, zr2, t1, d0, d1, xr0, xr1, pf0, pf1, xm, um,
           cs1, cs2, cr1, cr2, kept, mid, red_s, red_r, ssem, rsem, lssem, lrsem):
    bx, by, bz = block
    kx = reach
    me = [lax.axis_index(a) for a in AXES]
    ex, ey = bx + SPAN, by + 2 * EDGE
    mx, my = bx // 2 + 4, ey // 2
    qx = bx // 4
    lane = iota((ey, bz), 1)
    row = iota((ey, bz), 0)

    def valid(offset):
        ok = None
        for axis, step in enumerate(offset):
            if step == 0:
                continue
            place = me[axis] + step
            term = place >= 0 if step < 0 else place < counts[axis]
            ok = term if ok is None else jnp.logical_and(ok, term)
        return ok

    def target(offset):
        return tuple(m + s for m, s in zip(me, offset))

    near = [(dx, dy, dz) for dx in range(-kx, kx + 1) for dy in (-1, 0, 1) for dz in (-1, 0, 1)]
    near = [o for o in near if o != (0, 0, 0) and all(counts[a] > abs(o[a]) for a in range(3))]
    near.sort(key=lambda o: (-abs(o[0]), abs(o[1]) + abs(o[2])))
    close = [o for o in near if abs(o[0]) <= 1]

    barrier = pltpu.get_barrier_semaphore()
    lines = []
    for axis in range(3):
        for step in range(1, counts[axis]):
            to = list(me)
            to[axis] = lax.rem(me[axis] + step, counts[axis])
            lines.append((axis, step, tuple(to)))

    zr1[...] = jnp.zeros_like(zr1)
    gc0[...] = jnp.zeros_like(gc0)
    cr1[...] = jnp.zeros_like(cr1)

    for offset in near:
        @pl.when(valid(offset))
        def _(offset=offset):
            pl.semaphore_signal(barrier, inc=1, device_id=target(offset), device_id_type=MESH)
    for axis, step, to in lines:
        pl.semaphore_signal(barrier, inc=1, device_id=to, device_id_type=MESH)

    def options(axis, far):
        total = 1
        for step in range(1, far + 1):
            if counts[axis] > step:
                total = total + (me[axis] >= step).astype(jnp.int32)
                total = total + (me[axis] + step < counts[axis]).astype(jnp.int32)
        return total

    greeted = options(0, kx) * options(1, 1) * options(2, 1) - 1 + len(lines)

    strip = (lane[:by] < WIDTH) | (lane[:by] >= bz - WIDTH)

    def packed(planes):
        total = None
        for i, plane in enumerate(planes):
            piece = jnp.where(strip, plane, 0.0)
            if i > 0:
                piece = pltpu.roll(piece, SPAN * i, 1)
            total = piece if total is None else total + piece
        return total

    def fill(buf, pk, s, planes):
        for i, plane in enumerate(planes):
            buf[s, WIDTH + i, EDGE:EDGE + by, :] = plane
        pk[s] = packed(planes)

    def row_ends(dy):
        if dy == 0:
            return 0, by, EDGE
        if dy > 0:
            return by - EDGE, EDGE, 0
        return 0, EDGE, EDGE + by

    def fine_copy(phase, n, offset, buf, pk, zr):
        dx, dy, dz = offset
        start, size, goes = row_ends(dy)
        if dz == 0:
            if dx == 0:
                px, nx, tx = WIDTH, bx, WIDTH
            elif dx > 0:
                px, nx, tx = bx, WIDTH, 0
            else:
                px, nx, tx = WIDTH, WIDTH, WIDTH + bx
            src = buf.at[:, pl.ds(px, nx), pl.ds(EDGE + start, size), :]
            dst = buf.at[:, pl.ds(tx, nx), pl.ds(goes, size), :]
        else:
            side = 0 if dz > 0 else 1
            src = pk.at[:, pl.ds(start, size), :]
            dst = zr.at[side, 1 - dx, :, pl.ds(goes, size), :]
        return pltpu.make_async_remote_copy(
            src_ref=src, dst_ref=dst, send_sem=ssem.at[phase, n], recv_sem=rsem.at[phase, n],
            device_id=target(offset), device_id_type=MESH)

    def coarse_copy(phase, n, offset, cs, cr):
        dx, dy, dz = offset
        return pltpu.make_async_remote_copy(
            src_ref=cs, dst_ref=cr.at[kx - dx, 1 - dy, 1 - dz],
            send_sem=ssem.at[phase, n], recv_sem=rsem.at[phase, n],
            device_id=target(offset), device_id_type=MESH)

    def begin(make, offsets):
        for n, offset in enumerate(offsets):
            @pl.when(valid(offset))
            def _(n=n, offset=offset):
                make(n, offset).start()

    def arrive(make, offsets):
        for n, offset in enumerate(offsets):
            @pl.when(valid(tuple(-s for s in offset)))
            def _(n=n, offset=offset):
                make(n, offset).wait_recv()

    def leave(make, offsets):
        for n, offset in enumerate(offsets):
            @pl.when(valid(offset))
            def _(n=n, offset=offset):
                make(n, offset).wait_send()

    def line_copy(axis, step, to):
        n = sum(counts[:axis]) + step
        return pltpu.make_async_remote_copy(
            src_ref=red_s.at[axis], dst_ref=red_r.at[n], send_sem=lssem.at[n],
            recv_sem=lrsem.at[n], device_id=to, device_id_type=MESH)

    def line_begin(axis, value):
        red_s[axis] = value
        for a, step, to in lines:
            if a == axis:
                line_copy(a, step, to).start()

    def line_end(axis):
        value = red_s[axis]
        for a, step, to in lines:
            if a == axis:
                line_copy(a, step, to).wait_recv()
                value = value + red_r[sum(counts[:a]) + step]
        return value

    place = lax.rem(lane + WIDTH, bz)
    low = lax.rem(place, SPAN) < WIDTH
    band = (lane < WIDTH) | (lane >= bz - WIDTH)

    def spread(zr, s, t):
        for side in range(3):
            merged = jnp.where(low, zr[0, side, s], zr[1, side, s])
            if side == 0:
                todo = [(bx - WIDTH + i, i) for i in range(WIDTH)]
            elif side == 1:
                todo = [(i, WIDTH + i) for i in range(bx)]
            else:
                todo = [(i, WIDTH + bx + i) for i in range(WIDTH)]
            for i, e in todo:
                piece = merged if i == 0 else pltpu.roll(merged, (bz - SPAN * i) % bz, 1)
                t1[t, e] = jnp.where(band, piece, 0.0)

    first, last = lane == 0, lane == bz - 1

    def yz(a, b):
        sa = a + jnp.where(first, pltpu.roll(b, 1, 1), pltpu.roll(a, 1, 1))
        sb = b + jnp.where(first, pltpu.roll(a, 1, 1), pltpu.roll(b, 1, 1))
        sa = sa + jnp.where(last, pltpu.roll(b, bz - 1, 1), pltpu.roll(a, bz - 1, 1))
        sb = sb + jnp.where(last, pltpu.roll(a, bz - 1, 1), pltpu.roll(b, bz - 1, 1))
        sa = sa + pltpu.roll(sa, 1, 0) + pltpu.roll(sa, ey - 1, 0)
        sb = sb + pltpu.roll(sb, 1, 0) + pltpu.roll(sb, ey - 1, 0)
        return sa, sb

    def box(v):
        s = v + pltpu.roll(v, 1, 2) + pltpu.roll(v, v.shape[2] - 1, 2)
        s = s + pltpu.roll(s, 1, 1) + pltpu.roll(s, v.shape[1] - 1, 1)
        zero = jnp.zeros_like(s[:1])
        return s + jnp.concatenate([zero, s[:-1]], 0) + jnp.concatenate([s[1:], zero], 0)

    p_, q_ = iota((bz, bz), 0), iota((bz, bz), 1)
    down_a = jnp.where((p_ >> 1) == q_, 0.5, 0.0)
    down_b = jnp.where(((p_ + bz) >> 1) == q_, 0.5, 0.0)
    up_a = jnp.where((q_ >> 1) == p_, 1.0, 0.0)
    up_b = jnp.where(((q_ + bz) >> 1) == p_, 1.0, 0.0)
    quarter = bz // 4
    down_c = jnp.where((p_ < bz // 2) & ((p_ >> 1) == lax.rem(q_, quarter)), 0.5, 0.0)
    up_c = jnp.where(p_ == jnp.where(q_ < 3 * quarter, q_ >> 1, (q_ >> 1) + bz // 2), 1.0, 0.0)

    def restricted(of):
        for m in range(mx):
            a0, b0 = of(2 * m + 1)
            a1, b1 = of(2 * m + 2)
            xr0[m * ey:(m + 1) * ey, :] = a0 + a1
            xr1[m * ey:(m + 1) * ey, :] = b0 + b1
        n = mx * my
        a = xr0[pl.ds(0, n, stride=2), :] + xr0[pl.ds(1, n, stride=2), :]
        b = xr1[pl.ds(0, n, stride=2), :] + xr1[pl.ds(1, n, stride=2), :]
        return (dot(a, down_a) + dot(b, down_b)).reshape(mx, my, bz)

    turn = iota((my // 2, bz), 1) // quarter
    crow = iota((my // 2, bz), 0)

    def coarsened(v, lift):
        for m in range(qx):
            xm[m * my:(m + 1) * my, :] = v[2 + 2 * m] + v[3 + 2 * m]
        n = qx * my // 2
        a = xm[pl.ds(0, n, stride=2), :] + xm[pl.ds(1, n, stride=2), :]
        a = dot(a, down_c)
        rows = my // 2
        tile = a[:rows]
        for m in range(1, qx):
            tile = jnp.where(turn == m, a[m * rows:(m + 1) * rows], tile)
        return pltpu.roll(tile, 2 if lift else rows - 2, 0)

    xs = [x for x in range(-PART, qx + PART) if -kx * qx <= x < (kx + 1) * qx]

    def gathered(cr, cs, lifts):
        half = my // 4
        columns = {}
        for dx in sorted({x // qx for x in xs}):
            for dy in (-1, 0, 1):
                here = cs[...] if (dx, dy) == (0, 0) else cr[kx + dx, 1 + dy, 1]
                after = pltpu.roll(cr[kx + dx, 1 + dy, 2], quarter, 1)
                before = pltpu.roll(cr[kx + dx, 1 + dy, 0], 3 * quarter, 1)
                for m in range(qx):
                    tile = jnp.where(turn == (m + 1) % 4, after, here)
                    tile = jnp.where(turn == (m + 3) % 4, before, tile)
                    if m > 0:
                        tile = pltpu.roll(tile, bz - quarter * m, 1)
                    columns[dx * qx + m, dy] = tile
        arrays = []
        for lift in lifts:
            planes = []
            for x in xs:
                tiles = [columns[x, dy] for dy in (-1, 0, 1)]
                turned = [pltpu.roll(t, half, 0) for t in tiles]
                if lift:
                    tiles, turned = turned, tiles
                upper = jnp.where(crow < half, tiles[0], turned[1])
                lower = jnp.where(crow < half, tiles[2], 0.0)
                planes.append(jnp.concatenate([upper, lower], 0))
            arrays.append(jnp.stack(planes))
        return arrays

    def within(place, axis, size):
        place = place + me[axis] * size
        return (place >= 0) & (place < counts[axis] * size)

    g = [g_ref[i] for i in range(bx)]
    fill(gc0, pk1, 0, g)
    fill(gc0, pk1, 1, [c_ref[i] for i in range(bx)])
    for buf in (zr2, im0, cr2):
        buf[...] = jnp.zeros_like(buf)
    pl.semaphore_wait(barrier, greeted)
    make_a = lambda n, o: fine_copy(0, n, o, gc0, pk1, zr1)
    begin(make_a, close)
    arrive(make_a, close)
    spread(zr1, 0, 0)
    spread(zr1, 1, 1)

    in_y = within(row - EDGE, 1, by)
    in_z = band & within(jnp.where(lane < bz // 2, lane + bz, lane - bz), 2, bz)
    for i in range(ex):
        in_x = within(jnp.full((ey, bz), i - WIDTH, jnp.int32), 0, bx)
        d0[i] = jnp.where(in_y & in_x, relaxation / (26.0 + gc0[1, i]), 0.0)
        d1[i] = jnp.where(in_y & in_x & in_z, relaxation / (26.0 + t1[1, i]), 0.0)

    c1 = restricted(lambda i: (gc0[1, i], t1[1, i]))
    shape = (mx, my, bz)
    zl = iota(shape, 2)
    zl = jnp.where(zl < 3 * quarter, zl, zl - bz)
    inside = within(iota(shape, 0) - 2, 0, bx // 2) & within(iota(shape, 1) - 4, 1, by // 2)
    inside = inside & within(zl, 2, bz // 2)
    mid[0] = jnp.where(inside, relaxation / (26.0 + c1), 0.0)
    mid[1] = 27.0 + c1
    cs1[...] = coarsened(c1, True)

    def inverse2(c2):
        shape = c2.shape
        z = iota(shape, 2)
        z = jnp.where(z < 2 * quarter, z, z - bz)
        ok = within(iota(shape, 0) + xs[0], 0, qx) & within(iota(shape, 1) - 4, 1, by // 4)
        ok = ok & within(z, 2, quarter) & (z >= -quarter)
        return jnp.where(ok, relaxation / (26.0 + c2), 0.0)

    def cycle(g_at, make_b, cs, cr, hook, second, finish):
        def e0(i):
            a, b = g_at(i)
            return d0[i] * a, d1[i] * b

        sums = {}

        def remainder(i):
            for k in (i - 1, i, i + 1):
                if k not in sums:
                    sums[k] = yz(*e0(k))
            a, b = g_at(i)
            ea, eb = e0(i)
            ra = a - (27.0 + gc0[1, i]) * ea + sums[i - 1][0] + sums[i][0] + sums[i + 1][0]
            rb = b - (27.0 + t1[1, i]) * eb + sums[i - 1][1] + sums[i][1] + sums[i + 1][1]
            return ra, rb

        g1 = restricted(remainder)
        f = mid[0] * g1
        mid[2] = g1
        tile = coarsened(g1 - mid[1] * f + box(f), False)
        cs[...] = jnp.where(crow < my // 4, tile, cs1[...])
        begin(make_b, near)
        hook()
        arrive(make_b, near)
        if cr is cr1:
            g2, c2 = gathered(cr, cs, (False, True))
            kept[0] = inverse2(c2)
            kept[1] = 27.0 + c2
        else:
            g2, = gathered(cr, cs, (False,))
        inv, diag = kept[0], kept[1]
        e = inv * g2
        for sweep in range(SWEEPS - 1):
            e = e + inv * (g2 - diag * e + box(e))
        second()
        nq = qx + 2
        e = jnp.concatenate([e[xs.index(x)][None] if x in xs else jnp.zeros_like(e[:1])
                             for x in range(-1, qx + 1)], 0)
        e = pltpu.roll(e, my - 2, 1)[:, :my // 2].reshape(nq * my // 2, bz)
        u = dot(e, up_c)
        um[pl.ds(0, nq * my // 2, stride=2), :] = u
        um[pl.ds(1, nq * my // 2, stride=2), :] = u
        u = um[...].reshape(nq, my, bz)
        u = jnp.concatenate([u[(m - 2) // 2 + 1][None] for m in range(mx)], 0)
        g1 = mid[2]
        f = mid[0] * g1 + u
        f = f + mid[0] * (g1 - mid[1] * f + box(f))
        nm = mx - 2
        f = f[1:mx - 1].reshape(nm * my, bz)
        for pf, up in ((pf0, up_a), (pf1, up_b)):
            w = dot(f, up)
            pf[pl.ds(0, nm * my, stride=2), :] = w
            pf[pl.ds(1, nm * my, stride=2), :] = w

        def e1(i):
            m = (i - WIDTH) // 2 + 1
            a, b = e0(i)
            return a + pf0[m * ey:(m + 1) * ey, :], b + pf1[m * ey:(m + 1) * ey, :]

        sums1, sums2 = {}, {}
        e2 = {}
        for i in range(WIDTH - 1, WIDTH + bx + 1):
            for k in (i - 1, i, i + 1):
                if k not in sums1:
                    sums1[k] = yz(*e1(k))
            ga, gb = g_at(i)
            ea, eb = e1(i)
            s = [sums1[i - 1][t] + sums1[i][t] + sums1[i + 1][t] for t in range(2)]
            za = ea + d0[i] * (ga - (27.0 + gc0[1, i]) * ea + s[0])
            zb = eb + d1[i] * (gb - (27.0 + t1[1, i]) * eb + s[1])
            e2[i] = za[EDGE:EDGE + by]
            sums2[i] = yz(za, zb)[0][EDGE:EDGE + by]
            k = i - 1
            if k - 1 in sums2:
                out = (27.0 + c_ref[k - WIDTH]) * e2[k] - (sums2[k - 1] + sums2[k] + sums2[k + 1])
                finish(k - WIDTH, e2[k], out)

    gamma, delta = [], []
    images = []

    def finish1(i, e, out):
        pre_ref[i] = e
        images.append(out)
        gamma.append(g_ref[i] * e)
        delta.append(out * e)

    nothing = lambda: None
    make_b = lambda n, o: coarse_copy(1, n, o, cs1, cr1)
    cycle(lambda i: (gc0[0, i], t1[0, i]), make_b, cs1, cr1, nothing, nothing, finish1)

    for i in range(bx):
        img_ref[i] = images[i]
    fill(im0, pk2, 0, images)
    make_c = lambda n, o: fine_copy(2, n, o, im0, pk2, zr2)
    begin(make_c, close)
    gs = jnp.sum(sum(gamma[1:], gamma[0]), axis=0, keepdims=True)
    ds = jnp.sum(sum(delta[1:], delta[0]), axis=0, keepdims=True)
    line_begin(2, jnp.where(iota((8, bz), 0) == 0, gs, ds))
    arrive(make_c, close)
    spread(zr2, 0, 2)

    def hook():
        line_begin(1, line_end(2))

    def second():
        line_begin(0, line_end(1))

    def finish2(i, e, out):
        twice_ref[i] = e
        image_twice_ref[i] = out

    make_d = lambda n, o: coarse_copy(3, n, o, cs2, cr2)
    cycle(lambda i: (im0[0, i], t1[2, i]), make_d, cs2, cr2, hook, second, finish2)

    total = jnp.sum(line_end(0), axis=1, keepdims=True)
    alpha_ref[...] = jnp.broadcast_to(total[0:1] / total[1:2], alpha_ref.shape)
    leave(make_a, close)
    leave(make_b, near)
    leave(make_c, close)
    leave(make_d, near)
    for axis, step, to in lines:
        line_copy(axis, step, to).wait_send()


def solution(mesh):
    counts = tuple(mesh.shape[a] for a in AXES)

    def shards(right_side, coefficient):
        bx, by, bz = block = right_side.shape
        assert SPAN * bx <= bz and by == 16 and bx % 4 == 0
        kx = max(1, min(-(-PART // (bx // 4)), counts[0] - 1))
        ex, ey = bx + SPAN, by + 2 * EDGE
        mx, my = bx // 2 + 4, ey // 2
        qx = bx // 4
        most = (2 * kx + 1) * 9
        planes = qx + 2 * min(PART, kx * qx)
        f32 = jnp.float32
        out = jax.ShapeDtypeStruct(block, f32)
        vmem = pl.BlockSpec(memory_space=pltpu.VMEM)
        precond, image, twice, image_twice, alpha = pl.pallas_call(
            functools.partial(kernel, counts, block, kx),
            out_shape=[out] * 4 + [jax.ShapeDtypeStruct((1, 1, bz), f32)],
            in_specs=[vmem] * 2,
            out_specs=[vmem] * 5,
            scratch_shapes=[
                pltpu.VMEM((2, ex, ey, bz), f32),
                pltpu.VMEM((1, ex, ey, bz), f32),
                pltpu.VMEM((2, by, bz), f32),
                pltpu.VMEM((1, by, bz), f32),
                pltpu.VMEM((2, 3, 2, ey, bz), f32),
                pltpu.VMEM((2, 3, 1, ey, bz), f32),
                pltpu.VMEM((3, ex, ey, bz), f32),
                pltpu.VMEM((ex, ey, bz), f32),
                pltpu.VMEM((ex, ey, bz), f32),
                pltpu.VMEM((mx * ey, bz), f32),
                pltpu.VMEM((mx * ey, bz), f32),
                pltpu.VMEM(((mx - 2) * ey, bz), f32),
                pltpu.VMEM(((mx - 2) * ey, bz), f32),
                pltpu.VMEM((qx * my, bz), f32),
                pltpu.VMEM(((qx + 2) * my, bz), f32),
                pltpu.VMEM((my // 2, bz), f32),
                pltpu.VMEM((my // 2, bz), f32),
                pltpu.VMEM((2 * kx + 1, 3, 3, my // 2, bz), f32),
                pltpu.VMEM((2 * kx + 1, 3, 3, my // 2, bz), f32),
                pltpu.VMEM((2, planes, my, bz), f32),
                pltpu.VMEM((3, mx, my, bz), f32),
                pltpu.VMEM((3, 8, bz), f32),
                pltpu.VMEM((sum(counts), 8, bz), f32),
                pltpu.SemaphoreType.DMA((4, most)),
                pltpu.SemaphoreType.DMA((4, most)),
                pltpu.SemaphoreType.DMA((sum(counts),)),
                pltpu.SemaphoreType.DMA((sum(counts),)),
            ],
            compiler_params=pltpu.CompilerParams(collective_id=0, has_side_effects=True),
            name="relayed",
        )(right_side, coefficient)
        return (alpha * precond, right_side - alpha * image,
                precond - alpha * twice, image - alpha * image_twice)

    placed = (P(*AXES), P(*AXES))
    return jax.shard_map(
        shards, mesh=mesh, in_specs=placed, out_specs=(P(*AXES),) * 4, check_vma=False
    )
```

profile of v0, /device:TPU:0, one launch (start us, length us, event | category | flops | bytes accessed | tf_op | source)
XLA Modules:
  0.0 36.0 jit_solution(6003137607642590870)
XLA Ops:
  0.6 0.0 copy-start
  0.6 32.9 %relayed.1 = (f32[12,16,128]{2,1,0:T(8,128)}, f32[12,16,128]{2,1,0:T(8,128)}, f32[12,16,128]{2,1,0:T(8,128)}, f32[12,16,128]{2,1,0:T(8,128)}, f32[1,1,128]{2,1,0:T(1,128)}) custom-call(f32[12,16,128]{2,1,0:T(8,128)} %g_ref.1, f32[12,16,128]{2,1,0:T(8,128)} %c_ref.1), custom_call_target="tpu_custom_call" | custom-call | tf_op jit(solution)/shard_map/relayed/pallas_call | solution.py:460
  33.5 0.0 copy-start.1
  33.5 0.0 copy-done
  33.5 0.6 %copy-done.1 = f32[1,1,128]{2,1,0:T(1,128)S(1)} copy-done((f32[1,1,128]{2,1,0:T(1,128)S(1)}, f32[1,1,128]{2,1,0:T(1,128)}, u32[]{:S(2)}) %copy-start.1) | copy-done | bytes 536
  34.2 1.8 %multiply_subtract_fusion = (f32[12,16,128]{2,1,0:T(8,128)}, f32[12,16,128]{2,1,0:T(8,128)}, f32[12,16,128]{2,1,0:T(8,128)}, f32[12,16,128]{2,1,0:T(8,128)}) fusion(f32[12,16,128]{2,1,0:T(8,128)} %get-tuple-element.11, f32[12,16,128]{2,1,0:T(8,128)} %get-tuple-element.13, f32[128]{0:T(128)S(1)} %bitcast.1, f32[12,16,128]{2,1,0:T(8,128)S(1)} %copy-done, ...), kind=kLoop, calls=%fused_computation | loop fusion | flops 172032 | bytes 885248 | tf_op jit(solution)/shard_map/sub | solution.py:498
Async XLA Ops:
  0.6 32.9 %copy-start = (f32[12,16,128]{2,1,0:T(8,128)S(1)}, f32[12,16,128]{2,1,0:T(8,128)}, u32[]{:S(2)}) copy-start(f32[12,16,128]{2,1,0:T(8,128)} %g_ref.1) | copy-start | bytes 294916
  33.5 0.7 %copy-start.1 = (f32[1,1,128]{2,1,0:T(1,128)S(1)}, f32[1,1,128]{2,1,0:T(1,128)}, u32[]{:S(2)}) copy-start(f32[1,1,128]{2,1,0:T(1,128)} %get-tuple-element.9) | copy-start | bytes 1540
where the time goes:
time: 36.2 us; the launch traced here: 36 us
  Pallas kernels  32.9 us (91%)
  other arithmetic  1.78 us (5%)
  between operations  0.66 us (2%)
  local copies, waits for them, and re-layouts  0.65 us (2%)
    pallas_call x1, Pallas kernels, shards(): pl.pallas_call(functools.partial(kernel, counts, block, kx), out_shape=[o...  32.9 us
    sub x1, other arithmetic, shards(): image - alpha * image_twice  1.78 us

commit v1 on v0

--- a/solution.py
+++ b/solution.py
@@ -30,8 +30,8 @@
     return lax.broadcasted_iota(jnp.int32, shape, dim)
 
 
-def kernel(counts, block, reach, g_ref, c_ref, pre_ref, img_ref, twice_ref, image_twice_ref, alpha_ref,
-           gc0, im0, pk1, pk2, zr1, zr2, t1, d0, d1, xr0, xr1, pf0, pf1, xm, um,
+def kernel(counts, block, reach, g_hbm, c_hbm, pre_ref, img_ref, twice_ref, image_twice_ref, alpha_ref, g_ref,
+           c_ref, insem, gc0, im0, pk1, pk2, zr1, zr2, t1, d0, d1, xr0, xr1, pf0, pf1, xm, um,
            cs1, cs2, cr1, cr2, kept, mid, red_s, red_r, ssem, rsem, lssem, lrsem):
     bx, by, bz = block
     kx = reach
@@ -68,6 +68,10 @@
             to[axis] = lax.rem(me[axis] + step, counts[axis])
             lines.append((axis, step, tuple(to)))
 
+    copies = [pltpu.make_async_copy(src, dst, insem.at[n])
+              for n, (src, dst) in enumerate(((g_hbm, g_ref), (c_hbm, c_ref)))]
+    for copy in copies:
+        copy.start()
     zr1[...] = jnp.zeros_like(zr1)
     gc0[...] = jnp.zeros_like(gc0)
     cr1[...] = jnp.zeros_like(cr1)
@@ -280,6 +284,8 @@
         place = place + me[axis] * size
         return (place >= 0) & (place < counts[axis] * size)
 
+    for copy in copies:
+        copy.wait()
     g = [g_ref[i] for i in range(bx)]
     fill(gc0, pk1, 0, g)
     fill(gc0, pk1, 1, [c_ref[i] for i in range(bx)])
@@ -455,14 +461,15 @@
         most = (2 * kx + 1) * 9
         planes = qx + 2 * min(PART, kx * qx)
         f32 = jnp.float32
-        out = jax.ShapeDtypeStruct(block, f32)
         vmem = pl.BlockSpec(memory_space=pltpu.VMEM)
-        precond, image, twice, image_twice, alpha = pl.pallas_call(
+        precond, image, twice, image_twice, alpha, g = pl.pallas_call(
             functools.partial(kernel, counts, block, kx),
-            out_shape=[out] * 4 + [jax.ShapeDtypeStruct((1, 1, bz), f32)],
-            in_specs=[vmem] * 2,
-            out_specs=[vmem] * 5,
+            out_shape=[pltpu.VMEM(block, f32)] * 4 + [pltpu.VMEM((1, 1, bz), f32), pltpu.VMEM(block, f32)],
+            in_specs=[pl.BlockSpec(memory_space=pltpu.HBM)] * 2,
+            out_specs=[vmem] * 6,
             scratch_shapes=[
+                pltpu.VMEM(block, f32),
+                pltpu.SemaphoreType.DMA((2,)),
                 pltpu.VMEM((2, ex, ey, bz), f32),
                 pltpu.VMEM((1, ex, ey, bz), f32),
                 pltpu.VMEM((2, by, bz), f32),
@@ -494,7 +501,7 @@
             compiler_params=pltpu.CompilerParams(collective_id=0, has_side_effects=True),
             name="relayed",
         )(right_side, coefficient)
-        return (alpha * precond, right_side - alpha * image,
+        return (alpha * precond, g - alpha * image,
                 precond - alpha * twice, image - alpha * image_twice)
 
     placed = (P(*AXES), P(*AXES))

time: 36.2 us -> 32.7 us (0.903)
  Pallas kernels: 32.9 us -> 31.1 us
  other arithmetic: 1.78 us -> 0.76 us
  local copies, waits for them, and re-layouts: 0.65 us -> 0 us
    pallas_call x1, Pallas kernels: 32.9 us -> 31.1 us  [shards(): pl.pallas_call(functools.partial(kernel, counts, block, kx), out_shape=[p...]
    sub x1, other arithmetic: 1.78 us -> 0.76 us  [shards(): image - alpha * image_twice]
    unnamed x4 -> x0, local copies, waits for them, and re-layouts: 0.65 us -> none
where the time goes in v1:
time: 32.7 us; the launch traced here: 32.5 us
  Pallas kernels  31.1 us (95%)
  other arithmetic  0.76 us (2%)
  between operations  0.64 us (2%)
    pallas_call x1, Pallas kernels, shards(): pl.pallas_call(functools.partial(kernel, counts, block, kx), out_shape=[p...  31.1 us
    sub x1, other arithmetic, shards(): image - alpha * image_twice  0.76 us

profile of v1, /device:TPU:0, one launch (start us, length us, event | category | flops | bytes accessed | tf_op | source)
XLA Modules:
  0.0 32.5 jit_solution(14929394669797668709)
XLA Ops:
  0.6 31.1 %relayed.1 = (f32[12,16,128]{2,1,0:T(8,128)S(1)}, f32[12,16,128]{2,1,0:T(8,128)S(1)}, f32[12,16,128]{2,1,0:T(8,128)S(1)}, f32[12,16,128]{2,1,0:T(8,128)S(1)}, f3...) custom-call(f32[12,16,128]{2,1,0:T(8,128)} %g_hbm.1, f32[12,16,128]{2,1,0:T(8,128)} %c_hbm.1), custom_call_target="tpu_custom_call" | custom-call | tf_op jit(solution)/shard_map/relayed/pallas_call | solution.py:465
  31.8 0.8 %multiply_subtract_fusion = (f32[12,16,128]{2,1,0:T(8,128)}, f32[12,16,128]{2,1,0:T(8,128)}, f32[12,16,128]{2,1,0:T(8,128)}, f32[12,16,128]{2,1,0:T(8,128)}) fusion(f32[12,16,128]{2,1,0:T(8,128)S(1)} %get-tuple-element.13, f32[12,16,128]{2,1,0:T(8,128)S(1)} %get-tuple-element.15, f32[128]{0:T(128)S(1)} %bitcast.1, f32[12,16,128]{2,1,0:T(8,128)S(1)} %get-tuple-element.12, ...), kind=kLoop, calls=%fused_computation | loop fusion | flops 172032 | bytes 885248 | tf_op jit(solution)/shard_map/sub | solution.py:505

commit v2 on v1

v2 whole, which is shorter than its diff:
```python
import functools

import jax
import jax.numpy as jnp
from jax import lax
from jax.experimental import pallas as pl
from jax.experimental.pallas import tpu as pltpu
from jax.sharding import PartitionSpec as P

SWEEPS = 4
relaxation = 0.6

AXES = ("gx", "gy", "gz")
MESH = pl.DeviceIdType.MESH
WIDTH = 5
INNER = 3
EDGE = 8
SPAN = 2 * WIDTH
RIM = 4
PART = SWEEPS + 1


def dot(a, b):
    high = a.astype(jnp.bfloat16)
    low = (a - high.astype(jnp.float32)).astype(jnp.bfloat16)
    both = jnp.concatenate([high, low], 1)
    b = b.astype(jnp.bfloat16)
    return jnp.dot(both, jnp.concatenate([b, b], 0), preferred_element_type=jnp.float32)


def iota(shape, dim):
    return lax.broadcasted_iota(jnp.int32, shape, dim)


def total_of(values):
    while len(values) > 1:
        values = [a + b for a, b in zip(values[::2], values[1::2])] + values[len(values) & ~1:]
    return values[0]


def stages(counts):
    if max(counts) <= RIM:
        return [(0, 1, 2)]
    return [(2,), (1,), (0,)]


def partners(counts, group):
    steps = [(0, 0, 0)]
    for axis in group:
        steps = [s[:axis] + (k,) + s[axis + 1:] for s in steps for k in range(counts[axis])]
    return [s for s in steps if s != (0, 0, 0)]


def kernel(counts, block, kx, ky, g_hbm, c_hbm, pre_ref, img_ref, twice_ref, image_twice_ref, alpha_ref, g_ref,
           c_ref, gc0, im0, pk, pkx, zr, zrx, t1, d0, d1, xr0, xr1, pf0, pf1, xm, um,
           s0, s1, s2, r0, r1, r2, kept, mid, red_s, red_r, insem, ssem, rsem, lssem, lrsem):
    bx, by, bz = block
    me = [lax.axis_index(a) for a in AXES]
    ex, ey = bx + SPAN, by + 2 * EDGE
    ox, my = bx // 2, ey // 2
    qx, qy = bx // 4, by // 4
    half, quarter = bz // 2, bz // 4
    lane = iota((ey, bz), 1)
    row = iota((ey, bz), 0)
    lane8 = iota((8, bz), 1)
    row8 = iota((8, bz), 0)

    def valid(offset):
        ok = None
        for axis, step in enumerate(offset):
            if step == 0:
                continue
            place = me[axis] + step
            term = place >= 0 if step < 0 else place < counts[axis]
            ok = term if ok is None else jnp.logical_and(ok, term)
        return ok

    def target(offset):
        return tuple(m + s for m, s in zip(me, offset))

    near = [(dx, dy, dz) for dx in range(-kx, kx + 1) for dy in range(-ky, ky + 1) for dz in (-1, 0, 1)]
    near = [o for o in near if o != (0, 0, 0) and all(counts[a] > abs(o[a]) for a in range(3))]
    near.sort(key=lambda o: -sum(map(abs, o)))
    close = [o for o in near if abs(o[0]) <= 1 and abs(o[1]) <= 1]
    sides = [o for o in close if o[0] != 0 and o[2] == 0]
    later = [o for o in near if abs(o[1]) <= 1]

    groups = stages(counts)
    mates = []
    base = [0]
    for group in groups:
        mates.append(partners(counts, group))
        base.append(base[-1] + len(mates[-1]))

    def mate(step):
        return tuple(lax.rem(m + s, n) if s else m for m, s, n in zip(me, step, counts))

    copies = [pltpu.make_async_copy(src, dst, insem.at[n])
              for n, (src, dst) in enumerate(((g_hbm, g_ref), (c_hbm, c_ref)))]
    for copy in copies:
        copy.start()
    gc0[...] = jnp.zeros_like(gc0)
    zr[...] = jnp.zeros_like(zr)
    zrx[...] = jnp.zeros_like(zrx)

    barrier = pltpu.get_barrier_semaphore()
    for offset in near:
        @pl.when(valid(offset))
        def _(offset=offset):
            pl.semaphore_signal(barrier, inc=1, device_id=target(offset), device_id_type=MESH)
    greeted = 0
    if len(groups) > 1:
        for steps in mates:
            for step in steps:
                pl.semaphore_signal(barrier, inc=1, device_id=mate(step), device_id_type=MESH)
            greeted = greeted + len(steps)

    def options(axis, far):
        total = 1
        for step in range(1, far + 1):
            if counts[axis] > step:
                total = total + (me[axis] >= step).astype(jnp.int32)
                total = total + (me[axis] + step < counts[axis]).astype(jnp.int32)
        return total

    greeted = greeted + options(0, kx) * options(1, ky) * options(2, 1) - 1

    def row_ends(dy):
        if dy == 0:
            return 0, by, EDGE
        if dy > 0:
            return by - EDGE, EDGE, 0
        return 0, EDGE, EDGE + by

    def remote(src, dst, phase, n, offset):
        return pltpu.make_async_remote_copy(
            src_ref=src, dst_ref=dst, send_sem=ssem.at[phase, n], recv_sem=rsem.at[phase, n],
            device_id=target(offset), device_id_type=MESH)

    def planes_copy(phase, n, offset, first, size):
        dx, dy, dz = offset
        start, rows, goes = row_ends(dy)
        if dx == 0:
            px, tx, size = WIDTH, WIDTH, bx
        elif dx > 0:
            px, tx = WIDTH + bx - first - size, WIDTH - first - size
        else:
            px, tx = WIDTH + first, WIDTH + bx + first
        src = gc0.at[:, pl.ds(px, size), pl.ds(EDGE + start, rows), :]
        dst = gc0.at[:, pl.ds(tx, size), pl.ds(goes, rows), :]
        return remote(src, dst, phase, n, offset)

    def fine_copy(n, offset):
        dx, dy, dz = offset
        if dz == 0:
            return planes_copy(0, n, offset, 0, INNER)
        start, rows, goes = row_ends(dy)
        side = 0 if dz > 0 else 1
        if dx == 0:
            src = pk.at[:, pl.ds(start, rows), :]
            dst = zr.at[side, :, pl.ds(goes, rows), :]
        else:
            end = 0 if dx > 0 else 1
            src = pkx.at[end, pl.ds(start, rows), :]
            dst = zrx.at[side, end, pl.ds(goes, rows), :]
        return remote(src, dst, 0, n, offset)

    def outer_copy(n, offset):
        return planes_copy(1, n, offset, INNER, WIDTH - INNER)

    def part(offset, depth):
        dx, dy, dz = offset
        if abs(dx) > 1 or abs(dy) > 1:
            return 0, 1
        if dz != 0:
            return 4, 2
        if dx == 0:
            return 0, 4
        if dx < 0:
            return 0, 1 + depth
        return 4 - depth, 1 + depth

    def coarse_copy(phase, n, offset, s, r, depth):
        dx, dy, dz = offset
        at, size = part(offset, depth)
        return remote(s.at[pl.ds(at, size)], r.at[kx - dx, ky - dy, 1 - dz, pl.ds(at, size)], phase, n, offset)

    def begin(make, offsets):
        for n, offset in enumerate(offsets):
            @pl.when(valid(offset))
            def _(n=n, offset=offset):
                make(n, offset).start()

    def arrive(make, offsets):
        for n, offset in enumerate(offsets):
            @pl.when(valid(tuple(-s for s in offset)))
            def _(n=n, offset=offset):
                make(n, offset).wait_recv()

    def leave(make, offsets):
        for n, offset in enumerate(offsets):
            @pl.when(valid(offset))
            def _(n=n, offset=offset):
                make(n, offset).wait_send()

    def mate_copy(stage, k):
        n = base[stage] + k
        return pltpu.make_async_remote_copy(
            src_ref=red_s.at[stage], dst_ref=red_r.at[n], send_sem=lssem.at[n],
            recv_sem=lrsem.at[n], device_id=mate(mates[stage][k]), device_id_type=MESH)

    def sum_begin(stage, value):
        red_s[stage] = value
        for k in range(len(mates[stage])):
            mate_copy(stage, k).start()

    def sum_end(stage):
        for k in range(len(mates[stage])):
            mate_copy(stage, k).wait_recv()
        return total_of([red_s[stage]] + [red_r[base[stage] + k] for k in range(len(mates[stage]))])

    strip = (lane[:by] < WIDTH) | (lane[:by] >= bz - WIDTH)
    place = lax.rem(lane + WIDTH, bz)
    low = lax.rem(place, SPAN) < WIDTH
    band = (lane < WIDTH) | (lane >= bz - WIDTH)
    first, last = lane == 0, lane == bz - 1

    def turn_to(v, shift):
        shift = shift % bz
        return v if shift == 0 else pltpu.roll(v, shift, 1)

    def pack(planes):
        pieces = [turn_to(jnp.where(strip, plane, 0.0), SPAN * i) for i, plane in enumerate(planes)]
        ends = (total_of(pieces[bx - WIDTH:]), total_of(pieces[:WIDTH]))
        return ends, total_of(pieces[WIDTH:bx - WIDTH] + list(ends))

    def yz(a, b):
        sa = a + jnp.where(first, pltpu.roll(b, 1, 1), pltpu.roll(a, 1, 1))
        sb = b + jnp.where(first, pltpu.roll(a, 1, 1), pltpu.roll(b, 1, 1))
        sa = sa + jnp.where(last, pltpu.roll(b, bz - 1, 1), pltpu.roll(a, bz - 1, 1))
        sb = sb + jnp.where(last, pltpu.roll(a, bz - 1, 1), pltpu.roll(b, bz - 1, 1))
        sa = sa + pltpu.roll(sa, 1, 0) + pltpu.roll(sa, ey - 1, 0)
        sb = sb + pltpu.roll(sb, 1, 0) + pltpu.roll(sb, ey - 1, 0)
        return sa, sb

    def box(v):
        s = v + pltpu.roll(v, 1, 2) + pltpu.roll(v, v.shape[2] - 1, 2)
        s = s + pltpu.roll(s, 1, 1) + pltpu.roll(s, v.shape[1] - 1, 1)
        zero = jnp.zeros_like(s[:1])
        return s + jnp.concatenate([zero, s[:-1]], 0) + jnp.concatenate([s[1:], zero], 0)

    p_, q_ = iota((bz, bz), 0), iota((bz, bz), 1)
    down_a = jnp.where((p_ >> 1) == q_, 0.5, 0.0)
    down_b = jnp.where(((p_ + bz) >> 1) == q_, 0.5, 0.0)
    up_a = jnp.where((q_ >> 1) == p_, 1.0, 0.0)
    up_b = jnp.where(((q_ + bz) >> 1) == p_, 1.0, 0.0)
    down_c = jnp.where((p_ < half) & ((p_ >> 1) == lax.rem(q_, quarter)), 0.5, 0.0)
    up_c = jnp.where(p_ == jnp.where(q_ < 3 * quarter, q_ >> 1, (q_ >> 1) + half), 1.0, 0.0)

    lx = ox + 2

    def restricted(of):
        for m in range(lx):
            a0, b0 = of(2 * m + INNER)
            a1, b1 = of(2 * m + INNER + 1)
            xr0[m * ey:(m + 1) * ey, :] = a0 + a1
            xr1[m * ey:(m + 1) * ey, :] = b0 + b1
        n = lx * my
        a = xr0[pl.ds(0, n, stride=2), :] + xr0[pl.ds(1, n, stride=2), :]
        b = xr1[pl.ds(0, n, stride=2), :] + xr1[pl.ds(1, n, stride=2), :]
        return (dot(a, down_a) + dot(b, down_b)).reshape(lx, my, bz)

    turn = lane8 // quarter

    def coarsened(v):
        for m in range(qx):
            xm[m * my:(m + 1) * my, :] = v[2 * m] + v[2 * m + 1]
        n = qx * my // 2
        a = xm[pl.ds(0, n, stride=2), :] + xm[pl.ds(1, n, stride=2), :]
        a = dot(a, down_c)
        rows = my // 2
        tile = a[:rows]
        for m in range(1, qx):
            tile = jnp.where(turn == m, a[m * rows:(m + 1) * rows], tile)
        return pltpu.roll(tile, rows - 2, 0)

    rim = (lane8 < RIM) | ((lane8 >= half - RIM) & (lane8 < half))
    edge1 = my // 2 - by // 4

    def post(s, v1, tile):
        own = [v1[p][edge1:edge1 + by // 2] for p in range(ox)]
        s[0] = tile
        for k in range(ox // 2):
            s[1 + k] = jnp.where(lane8 < half, own[2 * k], pltpu.roll(own[2 * k + 1], half, 1))
        s[4] = tile
        s[5] = total_of([turn_to(jnp.where(rim, own[p], 0.0), RIM * p) for p in range(ox)])

    def middle(s, r, width):
        depth = RIM // 2 if width > 2 else 1

        def get(dx, dy, dz, k):
            if (dx, dy, dz) == (0, 0, 0):
                return s[k]
            if any(abs(d) >= n for d, n in zip((dx, dy, dz), counts)):
                return jnp.zeros((8, bz), jnp.float32)
            return r[kx + dx, ky + dy, 1 + dz, k]

        def rows(tiles):
            before, here, after = tiles
            return (pltpu.roll(jnp.where(row8 >= 4, before, here), 4, 0),
                    pltpu.roll(jnp.where(row8 >= 4, here, after), 4, 0))

        planes = []
        for dx in (-1, 0, 1):
            tiles = range(ox // 2 - depth, ox // 2) if dx < 0 else range(depth) if dx > 0 else range(ox // 2)
            ends = rows([jnp.where(lane8 < RIM * ox + RIM, get(dx, dy, 1, 5), get(dx, dy, -1, 5)) for dy in (-1, 0, 1)])
            for k in tiles:
                pair = rows([get(dx, dy, 0, 1 + k) for dy in (-1, 0, 1)])
                for odd in (0, 1):
                    p = 2 * k + odd
                    planes.append(jnp.concatenate([
                        jnp.where(lane8 < half, pltpu.roll(t, half, 1) if odd else t, turn_to(e, half - RIM * p))
                        for t, e in zip(pair, ends)], 0))
        return jnp.stack(planes)

    xs = [x for x in range(-PART, qx + PART) if -kx * qx <= x < (kx + 1) * qx]

    def gathered(s, r, far):
        zero = jnp.zeros((8, bz), jnp.float32)

        def get(dx, dy, dz):
            if (dx, dy, dz) == (0, 0, 0):
                return s[0]
            if any(abs(d) >= n for d, n in zip((dx, dy, dz), counts)) or abs(dy) > far:
                return zero
            return r[kx + dx, ky + dy, 1 + dz, part((-dx, -dy, -dz), 0)[0]]

        columns = {}
        for dx in sorted({x // qx for x in xs}):
            for dy in range(-2, 3):
                if abs(dy) > far:
                    continue
                here = get(dx, dy, 0)
                after = pltpu.roll(get(dx, dy, 1), quarter, 1)
                before = pltpu.roll(get(dx, dy, -1), 3 * quarter, 1)
                for m in range(qx):
                    tile = jnp.where(turn == (m + 1) % 4, after, here)
                    tile = jnp.where(turn == (m + 3) % 4, before, tile)
                    columns[dx * qx + m, dy] = turn_to(tile, -quarter * m)
        planes = []
        for x in xs:
            t = {dy: columns.get((x, dy), zero) for dy in range(-2, 3)}
            upper = jnp.where(row8 < qy, t[-1], pltpu.roll(t[0], 4, 0))
            if far > 1:
                lower = jnp.where(row8 < qy, t[1], pltpu.roll(jnp.where(row8 < 2, t[2], t[-2]), 4, 0))
            else:
                lower = jnp.where(row8 < qy, t[1], 0.0)
            planes.append(jnp.concatenate([upper, lower], 0))
        return jnp.stack(planes)

    def within(place, axis, size):
        place = place + me[axis] * size
        return (place >= 0) & (place < counts[axis] * size)

    for copy in copies:
        copy.wait()
    g = [g_ref[i] for i in range(bx)]
    c = [c_ref[i] for i in range(bx)]
    for i in range(bx):
        gc0[0, WIDTH + i, EDGE:EDGE + by, :] = g[i]
        gc0[1, WIDTH + i, EDGE:EDGE + by, :] = c[i]
    (g_last, g_first), pk[0] = pack(g)
    (c_last, c_first), pk[1] = pack(c)
    pkx[0] = g_last + turn_to(c_last, -SPAN * WIDTH)
    pkx[1] = g_first + turn_to(c_first, SPAN * WIDTH)
    pl.semaphore_wait(barrier, greeted)
    begin(fine_copy, close)

    for m in range(ox):
        xr0[m * ey + EDGE:m * ey + EDGE + by, :] = c[2 * m] + c[2 * m + 1]
    n = ox * my
    own1 = xr0[pl.ds(0, n, stride=2), :] + xr0[pl.ds(1, n, stride=2), :]
    own1 = dot(own1, down_a).reshape(ox, my, bz)
    post(s0, own1, coarsened(own1))
    make_c = lambda n, o: coarse_copy(2, n, o, s0, r0, RIM // 2)
    make_b = lambda n, o: coarse_copy(3, n, o, s1, r1, RIM // 2)
    make_d = lambda n, o: coarse_copy(4, n, o, s2, r2, 1)
    begin(outer_copy, sides)
    begin(make_c, near)

    in_y = within(row - EDGE, 1, by)
    in_z = band & within(jnp.where(lane < half, lane + bz, lane - bz), 2, bz)

    def spread(i):
        for f in range(2):
            if i < WIDTH:
                k = i
                piece = turn_to(ends[0], -SPAN * (bx - WIDTH + k - WIDTH * f))
            elif i >= WIDTH + bx:
                k = i - WIDTH - bx
                piece = turn_to(ends[1], -SPAN * (k + WIDTH * f))
            else:
                piece = turn_to(merged[f], -SPAN * (i - WIDTH))
            t1[f, i] = jnp.where(band, piece, 0.0)
        in_x = within(jnp.full((ey, bz), i - WIDTH, jnp.int32), 0, bx)
        d0[i] = jnp.where(in_y & in_x, relaxation / (26.0 + gc0[1, i]), 0.0)
        d1[i] = jnp.where(in_y & in_x & in_z, relaxation / (26.0 + t1[1, i]), 0.0)

    arrive(fine_copy, close)
    merged = [jnp.where(low, zr[0, f], zr[1, f]) for f in range(2)]
    ends = [jnp.where(low, zrx[0, e], zrx[1, e]) for e in range(2)]
    skip = WIDTH - INNER
    for i in range(skip, ex - skip):
        spread(i)

    def inside1(shape, width):
        zl = iota(shape, 2)
        zl = jnp.where(zl < 3 * quarter, zl, zl - bz)
        ok = within(iota(shape, 0) - width, 0, ox) & within(iota(shape, 1) - edge1, 1, by // 2)
        return ok & within(zl, 2, half) & (zl >= -RIM) & (zl < half + RIM)

    c1 = restricted(lambda i: (gc0[1, i], t1[1, i]))
    near0 = jnp.where(inside1((lx, my, bz), 1), relaxation / (26.0 + c1), 0.0)
    near1 = 27.0 + c1

    def coefficients():
        arrive(outer_copy, sides)
        for i in list(range(skip)) + list(range(ex - skip, ex)):
            spread(i)
        arrive(make_c, near)
        c1 = middle(s0, r0, RIM)
        ok = inside1(c1.shape, RIM)
        c1 = jnp.where(ok, c1, 0.0)
        mid[0] = jnp.where(ok, relaxation / (26.0 + c1), 0.0)
        mid[1] = 27.0 + c1
        c2 = gathered(s0, r0, ky)
        shape = c2.shape
        z = iota(shape, 2)
        z = jnp.where(z < 2 * quarter, z, z - bz)
        y = iota(shape, 1)
        y = jnp.where(y < my - 2, y, y - my) - qy
        ok = within(iota(shape, 0) + xs[0], 0, qx) & within(y, 1, qy)
        ok = ok & within(z, 2, quarter) & (z >= -quarter)
        c2 = jnp.where(ok, c2, 0.0)
        kept[0] = jnp.where(ok, relaxation / (26.0 + c2), 0.0)
        kept[1] = 27.0 + c2

    def cycle(g_at, near0, near1, s, r, make, offsets, far, width, hook, second, finish):
        def e0(i):
            a, b = g_at(i)
            return d0[i] * a, d1[i] * b

        sums = {}

        def remainder(i):
            for k in (i - 1, i, i + 1):
                if k not in sums:
                    sums[k] = yz(*e0(k))
            a, b = g_at(i)
            ea, eb = e0(i)
            ra = a - (27.0 + gc0[1, i]) * ea + sums[i - 1][0] + sums[i][0] + sums[i + 1][0]
            rb = b - (27.0 + t1[1, i]) * eb + sums[i - 1][1] + sums[i][1] + sums[i + 1][1]
            return ra, rb

        g1 = restricted(remainder)
        f = near0 * g1
        post(s, g1[1:1 + ox], coarsened((g1 - near1 * f + box(f))[1:1 + ox]))
        begin(make, offsets)
        hook()
        arrive(make, offsets)
        inv, diag = kept[0], kept[1]
        g2 = jnp.where(inv > 0.0, gathered(s, r, far), 0.0)
        e = inv * g2
        for sweep in range(SWEEPS - 1):
            e = e + inv * (g2 - diag * e + box(e))
        second()
        reach = (width + 1) // 2
        nq = qx + 2 * reach
        zero = jnp.zeros_like(e[:1])
        e = jnp.concatenate([e[xs.index(x)][None] if x in xs else zero for x in range(-reach, qx + reach)], 0)
        e = pltpu.roll(e, my - 2, 1)[:, :my // 2].reshape(nq * my // 2, bz)
        u = dot(e, up_c)
        um[pl.ds(0, nq * my // 2, stride=2), :] = u
        um[pl.ds(1, nq * my // 2, stride=2), :] = u
        u = um[:nq * my, :].reshape(nq, my, bz)
        span = width + 1
        mx = ox + 2 * span
        u = jnp.concatenate([u[(m - span) // 2 + reach][None] for m in range(mx)], 0)
        skip1 = RIM - span
        inv, diag = mid[0, skip1:skip1 + mx], mid[1, skip1:skip1 + mx]
        g1 = jnp.where(inv > 0.0, middle(s, r, span), 0.0)
        f = inv * g1 + u
        f = f + inv * (g1 - diag * f + box(f))
        nm = mx - 2
        f = f[1:mx - 1].reshape(nm * my, bz)
        for pf, up in ((pf0, up_a), (pf1, up_b)):
            w = dot(f, up)
            pf[pl.ds(0, nm * my, stride=2), :] = w
            pf[pl.ds(1, nm * my, stride=2), :] = w

        def e1(i):
            m = (i - WIDTH) // 2 + width
            a, b = e0(i)
            return a + pf0[m * ey:(m + 1) * ey, :], b + pf1[m * ey:(m + 1) * ey, :]

        sums1, sums2 = {}, {}
        e2 = {}
        wide = width > 1
        past = INNER + 1 if wide else 1
        for i in range(WIDTH - past, WIDTH + bx + past):
            for k in (i - 1, i, i + 1):
                if k not in sums1:
                    sums1[k] = yz(*e1(k))
            ga, gb = g_at(i)
            ea, eb = e1(i)
            s_ = [sums1[i - 1][t] + sums1[i][t] + sums1[i + 1][t] for t in range(2)]
            za = ea + d0[i] * (ga - (27.0 + gc0[1, i]) * ea + s_[0])
            zb = eb + d1[i] * (gb - (27.0 + t1[1, i]) * eb + s_[1])
            e2[i] = za, zb
            sums2[i] = yz(za, zb)
            k = i - 1
            if k - 1 in sums2:
                around = [sums2[k - 1][t] + sums2[k][t] + sums2[k + 1][t] for t in range(2)]
                za, zb = e2[k]
                finish(k, za, (27.0 + gc0[1, k]) * za - around[0],
                       (27.0 + t1[1, k]) * zb - around[1] if wide else None)

    gamma, delta = [], []

    def own(i):
        return WIDTH <= i < WIDTH + bx

    def finish1(i, e, out, out_b):
        im0[0, i] = out
        im0[1, i] = out_b
        if own(i):
            e, out = e[EDGE:EDGE + by], out[EDGE:EDGE + by]
            pre_ref[i - WIDTH] = e
            img_ref[i - WIDTH] = out
            gamma.append(g_ref[i - WIDTH] * e)
            delta.append(out * e)
        if i == WIDTH + bx - 1:
            gs = jnp.sum(total_of(gamma), axis=0, keepdims=True)
            ds = jnp.sum(total_of(delta), axis=0, keepdims=True)
            gs, ds = gs + pltpu.roll(gs, half, 1), ds + pltpu.roll(ds, half, 1)
            sum_begin(0, jnp.where(lane8[:1] < half, gs, ds))

    nothing = lambda: None
    cycle(lambda i: (gc0[0, i], t1[0, i]), near0, near1, s1, r1, make_b, near, ky, RIM - 1, coefficients, nothing, finish1)

    def relay(stage):
        if len(groups) > 1:
            sum_begin(stage, sum_end(stage - 1))

    def finish2(i, e, out, out_b):
        twice_ref[i - WIDTH] = e[EDGE:EDGE + by]
        image_twice_ref[i - WIDTH] = out[EDGE:EDGE + by]

    skip1 = RIM - 1
    cycle(lambda i: (im0[0, i], im0[1, i]), mid[0, skip1:skip1 + lx], mid[1, skip1:skip1 + lx], s2, r2, make_d, later, 1, 1,
          lambda: relay(1), lambda: relay(2), finish2)

    total = sum_end(len(groups) - 1)
    gs = jnp.sum(jnp.where(lane8[:1] < half, total, 0.0), axis=1, keepdims=True)
    ds = jnp.sum(jnp.where(lane8[:1] < half, 0.0, total), axis=1, keepdims=True)
    alpha_ref[...] = jnp.broadcast_to(gs / ds, (1, bz)).reshape(alpha_ref.shape)
    leave(fine_copy, close)
    leave(outer_copy, sides)
    leave(make_c, near)
    leave(make_b, near)
    leave(make_d, later)
    for stage in range(len(groups)):
        for k in range(len(mates[stage])):
            mate_copy(stage, k).wait_send()


def solution(mesh):
    counts = tuple(mesh.shape[a] for a in AXES)

    def shards(right_side, coefficient):
        bx, by, bz = block = right_side.shape
        assert SPAN <= bx and SPAN * bx <= bz and by == 16 and bx % 4 == 0
        kx = max(1, min(-(-PART // (bx // 4)), counts[0] - 1))
        ky = max(1, min(-(-PART // (by // 4)), counts[1] - 1))
        ex, ey = bx + SPAN, by + 2 * EDGE
        ox, my = bx // 2, ey // 2
        qx = bx // 4
        mx = ox + 2 * RIM
        most = (2 * kx + 1) * (2 * ky + 1) * 3
        planes = len([x for x in range(-PART, qx + PART) if -kx * qx <= x < (kx + 1) * qx])
        mates = [len(partners(counts, group)) for group in stages(counts)]
        f32 = jnp.float32
        vmem = pl.BlockSpec(memory_space=pltpu.VMEM)
        messages = [pltpu.VMEM((6, 8, bz), f32)] * 3
        messages += [pltpu.VMEM((2 * kx + 1, 2 * ky + 1, 3, 6, 8, bz), f32)] * 3
        precond, image, twice, image_twice, alpha, g = pl.pallas_call(
            functools.partial(kernel, counts, block, kx, ky),
            out_shape=[pltpu.VMEM(block, f32)] * 4 + [pltpu.VMEM((1, 1, bz), f32), pltpu.VMEM(block, f32)],
            in_specs=[pl.BlockSpec(memory_space=pltpu.HBM)] * 2,
            out_specs=[vmem] * 6,
            scratch_shapes=[
                pltpu.VMEM(block, f32),
                pltpu.VMEM((2, ex, ey, bz), f32),
                pltpu.VMEM((2, ex, ey, bz), f32),
                pltpu.VMEM((2, by, bz), f32),
                pltpu.VMEM((2, by, bz), f32),
                pltpu.VMEM((2, 2, ey, bz), f32),
                pltpu.VMEM((2, 2, ey, bz), f32),
                pltpu.VMEM((2, ex, ey, bz), f32),
                pltpu.VMEM((ex, ey, bz), f32),
                pltpu.VMEM((ex, ey, bz), f32),
                pltpu.VMEM(((ox + 2) * ey, bz), f32),
                pltpu.VMEM(((ox + 2) * ey, bz), f32),
                pltpu.VMEM(((mx - 2) * ey, bz), f32),
                pltpu.VMEM(((mx - 2) * ey, bz), f32),
                pltpu.VMEM((qx * my, bz), f32),
                pltpu.VMEM(((qx + 4) * my, bz), f32),
                *messages,
                pltpu.VMEM((2, planes, my, bz), f32),
                pltpu.VMEM((2, mx, my, bz), f32),
                pltpu.VMEM((len(mates), 1, bz), f32),
                pltpu.VMEM((sum(mates), 1, bz), f32),
                pltpu.SemaphoreType.DMA((2,)),
                pltpu.SemaphoreType.DMA((5, most)),
                pltpu.SemaphoreType.DMA((5, most)),
                pltpu.SemaphoreType.DMA((sum(mates),)),
                pltpu.SemaphoreType.DMA((sum(mates),)),
            ],
            compiler_params=pltpu.CompilerParams(collective_id=0, has_side_effects=True),
            name="relayed",
        )(right_side, coefficient)
        return (alpha * precond, g - alpha * image,
                precond - alpha * twice, image - alpha * image_twice)

    placed = (P(*AXES), P(*AXES))
    return jax.shard_map(
        shards, mesh=mesh, in_specs=placed, out_specs=(P(*AXES),) * 4, check_vma=False
    )
```

time: 32.7 us -> 30.2 us (0.924)
  Pallas kernels: 31.1 us -> 28.6 us
    pallas_call x1, Pallas kernels: 31.1 us -> 28.6 us  [shards(): pl.pallas_call(functools.partial(kernel, counts, block, kx, ky), out_shap...]
where the time goes in v2:
time: 30.2 us; the launch traced here: 30 us
  Pallas kernels  28.6 us (95%)
  other arithmetic  0.76 us (3%)
  between operations  0.64 us (2%)
    pallas_call x1, Pallas kernels, shards(): pl.pallas_call(functools.partial(kernel, counts, block, kx, ky), out_shap...  28.6 us
    sub x1, other arithmetic, shards(): image - alpha * image_twice  0.76 us

profile of v2, /device:TPU:0, one launch (start us, length us, event | category | flops | bytes accessed | tf_op | source)
XLA Modules:
  0.0 30.0 jit_solution(8634606844709380036)
XLA Ops:
  0.6 28.6 %relayed.1 = (f32[12,16,128]{2,1,0:T(8,128)S(1)}, f32[12,16,128]{2,1,0:T(8,128)S(1)}, f32[12,16,128]{2,1,0:T(8,128)S(1)}, f32[12,16,128]{2,1,0:T(8,128)S(1)}, f3...) custom-call(f32[12,16,128]{2,1,0:T(8,128)} %g_hbm.1, f32[12,16,128]{2,1,0:T(8,128)} %c_hbm.1), custom_call_target="tpu_custom_call" | custom-call | tf_op jit(solution)/shard_map/relayed/pallas_call | solution.py:596
  29.3 0.8 %multiply_subtract_fusion = (f32[12,16,128]{2,1,0:T(8,128)}, f32[12,16,128]{2,1,0:T(8,128)}, f32[12,16,128]{2,1,0:T(8,128)}, f32[12,16,128]{2,1,0:T(8,128)}) fusion(f32[12,16,128]{2,1,0:T(8,128)S(1)} %get-tuple-element.13, f32[12,16,128]{2,1,0:T(8,128)S(1)} %get-tuple-element.15, f32[128]{0:T(128)S(1)} %bitcast.1, f32[12,16,128]{2,1,0:T(8,128)S(1)} %get-tuple-element.12, ...), kind=kLoop, calls=%fused_computation | loop fusion | flops 172032 | bytes 885248 | tf_op jit(solution)/shard_map/sub | solution.py:633

commit v3 on v2

--- a/solution.py
+++ b/solution.py
@@ -1,4 +1,5 @@
 import functools
+import itertools
 
 import jax
 import jax.numpy as jnp
@@ -53,7 +54,7 @@
 
 def kernel(counts, block, kx, ky, g_hbm, c_hbm, pre_ref, img_ref, twice_ref, image_twice_ref, alpha_ref, g_ref,
            c_ref, gc0, im0, pk, pkx, zr, zrx, t1, d0, d1, xr0, xr1, pf0, pf1, xm, um,
-           s0, s1, s2, r0, r1, r2, kept, mid, red_s, red_r, insem, ssem, rsem, lssem, lrsem):
+           s0, s1, s2, r0, r1, r2, kept, mid, red_s, red_r, units, insem, ssem, rsem, lssem, lrsem):
     bx, by, bz = block
     me = [lax.axis_index(a) for a in AXES]
     ex, ey = bx + SPAN, by + 2 * EDGE
@@ -132,12 +133,12 @@
             return by - EDGE, EDGE, 0
         return 0, EDGE, EDGE + by
 
-    def remote(src, dst, phase, n, offset):
-        return pltpu.make_async_remote_copy(
-            src_ref=src, dst_ref=dst, send_sem=ssem.at[phase, n], recv_sem=rsem.at[phase, n],
-            device_id=target(offset), device_id_type=MESH)
-
-    def planes_copy(phase, n, offset, first, size):
+    def remote(src, dst, phase, offset):
+        pltpu.make_async_remote_copy(
+            src_ref=src, dst_ref=dst, send_sem=ssem, recv_sem=rsem.at[phase],
+            device_id=target(offset), device_id_type=MESH).start()
+
+    def planes_copy(phase, offset, first, size):
         dx, dy, dz = offset
         start, rows, goes = row_ends(dy)
         if dx == 0:
@@ -148,12 +149,12 @@
             px, tx = WIDTH + first, WIDTH + bx + first
         src = gc0.at[:, pl.ds(px, size), pl.ds(EDGE + start, rows), :]
         dst = gc0.at[:, pl.ds(tx, size), pl.ds(goes, rows), :]
-        return remote(src, dst, phase, n, offset)
-
-    def fine_copy(n, offset):
+        return (src, dst, phase, offset)
+
+    def fine_copy(offset):
         dx, dy, dz = offset
         if dz == 0:
-            return planes_copy(0, n, offset, 0, INNER)
+            return planes_copy(0, offset, 0, INNER)
         start, rows, goes = row_ends(dy)
         side = 0 if dz > 0 else 1
         if dx == 0:
@@ -163,10 +164,10 @@
             end = 0 if dx > 0 else 1
             src = pkx.at[end, pl.ds(start, rows), :]
             dst = zrx.at[side, end, pl.ds(goes, rows), :]
-        return remote(src, dst, 0, n, offset)
-
-    def outer_copy(n, offset):
-        return planes_copy(1, n, offset, INNER, WIDTH - INNER)
+        return (src, dst, 0, offset)
+
+    def outer_copy(offset):
+        return planes_copy(1, offset, INNER, WIDTH - INNER)
 
     def part(offset, depth):
         dx, dy, dz = offset
@@ -180,34 +181,71 @@
             return 0, 1 + depth
         return 4 - depth, 1 + depth
 
-    def coarse_copy(phase, n, offset, s, r, depth):
+    def coarse_copy(phase, offset, s, r, depth):
         dx, dy, dz = offset
         at, size = part(offset, depth)
-        return remote(s.at[pl.ds(at, size)], r.at[kx - dx, ky - dy, 1 - dz, pl.ds(at, size)], phase, n, offset)
+        return (s.at[pl.ds(at, size)], r.at[kx - dx, ky - dy, 1 - dz, pl.ds(at, size)], phase, offset)
+
+    def tiles(make, offset):
+        size = 1
+        for n in make(offset)[0].shape:
+            size *= n
+        assert size % (8 * bz) == 0
+        return size // (8 * bz)
 
     def begin(make, offsets):
-        for n, offset in enumerate(offsets):
+        for offset in offsets:
             @pl.when(valid(offset))
-            def _(n=n, offset=offset):
-                make(n, offset).start()
-
-    def arrive(make, offsets):
-        for n, offset in enumerate(offsets):
-            @pl.when(valid(tuple(-s for s in offset)))
-            def _(n=n, offset=offset):
-                make(n, offset).wait_recv()
-
-    def leave(make, offsets):
-        for n, offset in enumerate(offsets):
-            @pl.when(valid(offset))
-            def _(n=n, offset=offset):
-                make(n, offset).wait_send()
+            def _(offset=offset):
+                remote(*make(offset))
+
+    def wait_for(sem, pairs):
+        sizes = {}
+        for make, offsets in pairs:
+            for offset in offsets:
+                key = tuple(map(abs, offset))
+                sizes.setdefault(key, 0)
+                if offset == key:
+                    sizes[key] += tiles(make, offset)
+
+        def amount(options):
+            total = 0
+            for (a, b, c), size in sizes.items():
+                total = total + size * options[0][a] * options[1][b] * options[2][c]
+            return total
+
+        def number(place, count, step):
+            return 1 if step == 0 else (place >= step) * 1 + (place + step < count) * 1
+
+        def table(axis, place):
+            return [number(place, counts[axis], k) for k in range(3)]
+
+        here = []
+        for axis in range(3):
+            has = [1]
+            for k in (1, 2):
+                n = (me[axis] >= k).astype(jnp.int32) + (me[axis] + k < counts[axis]).astype(jnp.int32)
+                has.append(n)
+            here.append(has)
+        total = amount(here)
+        for value in sorted({amount(options) for options in itertools.product(
+                *[[table(axis, place) for place in range(counts[axis])] for axis in range(3)])}):
+            @pl.when(total == value)
+            def _(value=value):
+                some = units.at[pl.ds(0, value)]
+                pltpu.make_async_copy(some, some, sem).wait()
+
+    def arrive(phase, make, offsets):
+        wait_for(rsem.at[phase], [(make, offsets)])
+
+    def leave(pairs):
+        wait_for(ssem, pairs)
 
     def mate_copy(stage, k):
         n = base[stage] + k
         return pltpu.make_async_remote_copy(
-            src_ref=red_s.at[stage], dst_ref=red_r.at[n], send_sem=lssem.at[n],
-            recv_sem=lrsem.at[n], device_id=mate(mates[stage][k]), device_id_type=MESH)
+            src_ref=red_s.at[stage], dst_ref=red_r.at[n], send_sem=lssem.at[stage],
+            recv_sem=lrsem.at[stage], device_id=mate(mates[stage][k]), device_id_type=MESH)
 
     def sum_begin(stage, value):
         red_s[stage] = value
@@ -215,8 +253,8 @@
             mate_copy(stage, k).start()
 
     def sum_end(stage):
-        for k in range(len(mates[stage])):
-            mate_copy(stage, k).wait_recv()
+        some = red_r.at[pl.ds(base[stage], len(mates[stage]))]
+        pltpu.make_async_copy(some, some, lrsem.at[stage]).wait()
         return total_of([red_s[stage]] + [red_r[base[stage] + k] for k in range(len(mates[stage]))])
 
     strip = (lane[:by] < WIDTH) | (lane[:by] >= bz - WIDTH)
@@ -382,9 +420,9 @@
     own1 = xr0[pl.ds(0, n, stride=2), :] + xr0[pl.ds(1, n, stride=2), :]
     own1 = dot(own1, down_a).reshape(ox, my, bz)
     post(s0, own1, coarsened(own1))
-    make_c = lambda n, o: coarse_copy(2, n, o, s0, r0, RIM // 2)
-    make_b = lambda n, o: coarse_copy(3, n, o, s1, r1, RIM // 2)
-    make_d = lambda n, o: coarse_copy(4, n, o, s2, r2, 1)
+    make_c = lambda o: coarse_copy(2, o, s0, r0, RIM // 2)
+    make_b = lambda o: coarse_copy(3, o, s1, r1, RIM // 2)
+    make_d = lambda o: coarse_copy(4, o, s2, r2, 1)
     begin(outer_copy, sides)
     begin(make_c, near)
 
@@ -406,7 +444,7 @@
         d0[i] = jnp.where(in_y & in_x, relaxation / (26.0 + gc0[1, i]), 0.0)
         d1[i] = jnp.where(in_y & in_x & in_z, relaxation / (26.0 + t1[1, i]), 0.0)
 
-    arrive(fine_copy, close)
+    arrive(0, fine_copy, close)
     merged = [jnp.where(low, zr[0, f], zr[1, f]) for f in range(2)]
     ends = [jnp.where(low, zrx[0, e], zrx[1, e]) for e in range(2)]
     skip = WIDTH - INNER
@@ -424,10 +462,10 @@
     near1 = 27.0 + c1
 
     def coefficients():
-        arrive(outer_copy, sides)
+        arrive(1, outer_copy, sides)
         for i in list(range(skip)) + list(range(ex - skip, ex)):
             spread(i)
-        arrive(make_c, near)
+        arrive(2, make_c, near)
         c1 = middle(s0, r0, RIM)
         ok = inside1(c1.shape, RIM)
         c1 = jnp.where(ok, c1, 0.0)
@@ -445,7 +483,7 @@
         kept[0] = jnp.where(ok, relaxation / (26.0 + c2), 0.0)
         kept[1] = 27.0 + c2
 
-    def cycle(g_at, near0, near1, s, r, make, offsets, far, width, hook, second, finish):
+    def cycle(phase, g_at, near0, near1, s, r, make, offsets, far, width, hook, second, finish):
         def e0(i):
             a, b = g_at(i)
             return d0[i] * a, d1[i] * b
@@ -467,7 +505,7 @@
         post(s, g1[1:1 + ox], coarsened((g1 - near1 * f + box(f))[1:1 + ox]))
         begin(make, offsets)
         hook()
-        arrive(make, offsets)
+        arrive(phase, make, offsets)
         inv, diag = kept[0], kept[1]
         g2 = jnp.where(inv > 0.0, gathered(s, r, far), 0.0)
         e = inv * g2
@@ -546,7 +584,7 @@
             sum_begin(0, jnp.where(lane8[:1] < half, gs, ds))
 
     nothing = lambda: None
-    cycle(lambda i: (gc0[0, i], t1[0, i]), near0, near1, s1, r1, make_b, near, ky, RIM - 1, coefficients, nothing, finish1)
+    cycle(3, lambda i: (gc0[0, i], t1[0, i]), near0, near1, s1, r1, make_b, near, ky, RIM - 1, coefficients, nothing, finish1)
 
     def relay(stage):
         if len(groups) > 1:
@@ -557,21 +595,17 @@
         image_twice_ref[i - WIDTH] = out[EDGE:EDGE + by]
 
     skip1 = RIM - 1
-    cycle(lambda i: (im0[0, i], im0[1, i]), mid[0, skip1:skip1 + lx], mid[1, skip1:skip1 + lx], s2, r2, make_d, later, 1, 1,
+    cycle(4, lambda i: (im0[0, i], im0[1, i]), mid[0, skip1:skip1 + lx], mid[1, skip1:skip1 + lx], s2, r2, make_d, later, 1, 1,
           lambda: relay(1), lambda: relay(2), finish2)
 
     total = sum_end(len(groups) - 1)
     gs = jnp.sum(jnp.where(lane8[:1] < half, total, 0.0), axis=1, keepdims=True)
     ds = jnp.sum(jnp.where(lane8[:1] < half, 0.0, total), axis=1, keepdims=True)
     alpha_ref[...] = jnp.broadcast_to(gs / ds, (1, bz)).reshape(alpha_ref.shape)
-    leave(fine_copy, close)
-    leave(outer_copy, sides)
-    leave(make_c, near)
-    leave(make_b, near)
-    leave(make_d, later)
+    leave([(fine_copy, close), (outer_copy, sides), (make_c, near), (make_b, near), (make_d, later)])
     for stage in range(len(groups)):
-        for k in range(len(mates[stage])):
-            mate_copy(stage, k).wait_send()
+        some = red_r.at[pl.ds(base[stage], len(mates[stage]))]
+        pltpu.make_async_copy(some, some, lssem.at[stage]).wait()
 
 
 def solution(mesh):
@@ -620,11 +654,12 @@
                 pltpu.VMEM((2, mx, my, bz), f32),
                 pltpu.VMEM((len(mates), 1, bz), f32),
                 pltpu.VMEM((sum(mates), 1, bz), f32),
+                pltpu.VMEM((16 * most, 8, bz), f32),
                 pltpu.SemaphoreType.DMA((2,)),
-                pltpu.SemaphoreType.DMA((5, most)),
-                pltpu.SemaphoreType.DMA((5, most)),
-                pltpu.SemaphoreType.DMA((sum(mates),)),
-                pltpu.SemaphoreType.DMA((sum(mates),)),
+                pltpu.SemaphoreType.DMA,
+                pltpu.SemaphoreType.DMA((5,)),
+                pltpu.SemaphoreType.DMA((len(mates),)),
+                pltpu.SemaphoreType.DMA((len(mates),)),
             ],
             compiler_params=pltpu.CompilerParams(collective_id=0, has_side_effects=True),
             name="relayed",

time: 30.2 us -> 25.3 us (0.84)
  Pallas kernels: 28.6 us -> 23.7 us
    pallas_call x1, Pallas kernels: 28.6 us -> 23.7 us  [shards(): pl.pallas_call(functools.partial(kernel, counts, block, kx, ky), out_shap...]
where the time goes in v3:
time: 25.3 us; the launch traced here: 25.1 us
  Pallas kernels  23.7 us (94%)
  other arithmetic  0.76 us (3%)
  between operations  0.64 us (3%)
    pallas_call x1, Pallas kernels, shards(): pl.pallas_call(functools.partial(kernel, counts, block, kx, ky), out_shap...  23.7 us
    sub x1, other arithmetic, shards(): image - alpha * image_twice  0.76 us

profile of v3, /device:TPU:0, one launch (start us, length us, event | category | flops | bytes accessed | tf_op | source)
XLA Modules:
  0.0 25.1 jit_solution(5341951634985834818)
XLA Ops:
  0.6 23.7 %relayed.1 = (f32[12,16,128]{2,1,0:T(8,128)S(1)}, f32[12,16,128]{2,1,0:T(8,128)S(1)}, f32[12,16,128]{2,1,0:T(8,128)S(1)}, f32[12,16,128]{2,1,0:T(8,128)S(1)}, f3...) custom-call(f32[12,16,128]{2,1,0:T(8,128)} %g_hbm.1, f32[12,16,128]{2,1,0:T(8,128)} %c_hbm.1), custom_call_target="tpu_custom_call" | custom-call | tf_op jit(solution)/shard_map/relayed/pallas_call | solution.py:630
  24.4 0.8 %multiply_subtract_fusion = (f32[12,16,128]{2,1,0:T(8,128)}, f32[12,16,128]{2,1,0:T(8,128)}, f32[12,16,128]{2,1,0:T(8,128)}, f32[12,16,128]{2,1,0:T(8,128)}) fusion(f32[12,16,128]{2,1,0:T(8,128)S(1)} %get-tuple-element.13, f32[12,16,128]{2,1,0:T(8,128)S(1)} %get-tuple-element.15, f32[128]{0:T(128)S(1)} %bitcast.1, f32[12,16,128]{2,1,0:T(8,128)S(1)} %get-tuple-element.12, ...), kind=kLoop, calls=%fused_computation | loop fusion | flops 172032 | bytes 885248 | tf_op jit(solution)/shard_map/sub | solution.py:668

commit v4 on v3

--- a/solution.py
+++ b/solution.py
@@ -53,7 +53,7 @@
 
 
 def kernel(counts, block, kx, ky, g_hbm, c_hbm, pre_ref, img_ref, twice_ref, image_twice_ref, alpha_ref, g_ref,
-           c_ref, gc0, im0, pk, pkx, zr, zrx, t1, d0, d1, xr0, xr1, pf0, pf1, xm, um,
+           gc0, im0, pk, pkx, zr, zrx, t1, d0, d1, xr0, xr1, pf0, pf1, xm, um,
            s0, s1, s2, r0, r1, r2, kept, mid, red_s, red_r, units, insem, ssem, rsem, lssem, lrsem):
     bx, by, bz = block
     me = [lax.axis_index(a) for a in AXES]
@@ -96,14 +96,10 @@
     def mate(step):
         return tuple(lax.rem(m + s, n) if s else m for m, s, n in zip(me, step, counts))
 
-    copies = [pltpu.make_async_copy(src, dst, insem.at[n])
-              for n, (src, dst) in enumerate(((g_hbm, g_ref), (c_hbm, c_ref)))]
+    inside0 = gc0.at[:, pl.ds(WIDTH, bx), pl.ds(EDGE, by), :]
+    copies = [pltpu.make_async_copy(src, inside0.at[n], insem.at[n]) for n, src in enumerate((g_hbm, c_hbm))]
     for copy in copies:
         copy.start()
-    gc0[...] = jnp.zeros_like(gc0)
-    zr[...] = jnp.zeros_like(zr)
-    zrx[...] = jnp.zeros_like(zrx)
-
     barrier = pltpu.get_barrier_semaphore()
     for offset in near:
         @pl.when(valid(offset))
@@ -125,6 +121,19 @@
         return total
 
     greeted = greeted + options(0, kx) * options(1, ky) * options(2, 1) - 1
+
+    def clear(ref):
+        ref[...] = jnp.zeros(ref.shape, jnp.float32)
+
+    for axis, edges in enumerate((
+            [[gc0.at[:, pl.ds(0, WIDTH)], zrx.at[:, 0]], [gc0.at[:, pl.ds(WIDTH + bx, WIDTH)], zrx.at[:, 1]]],
+            [[ref.at[..., pl.ds(at, EDGE), :] for ref in (gc0, zr, zrx)] for at in (0, EDGE + by)],
+            [[ref.at[side] for ref in (zr, zrx)] for side in range(2)])):
+        for refs, edge in zip(edges, (0, counts[axis] - 1)):
+            @pl.when(me[axis] == edge)
+            def _(refs=refs):
+                for ref in refs:
+                    clear(ref)
 
     def row_ends(dy):
         if dy == 0:
@@ -174,7 +183,7 @@
         if abs(dx) > 1 or abs(dy) > 1:
             return 0, 1
         if dz != 0:
-            return 4, 2
+            return 4, 1
         if dx == 0:
             return 0, 4
         if dx < 0:
@@ -324,14 +333,17 @@
 
     rim = (lane8 < RIM) | ((lane8 >= half - RIM) & (lane8 < half))
     edge1 = my // 2 - by // 4
+    here_ends = (lane8 < RIM * ox) | ((lane8 >= half - RIM) & (lane8 < half - RIM + RIM * ox))
 
     def post(s, v1, tile):
         own = [v1[p][edge1:edge1 + by // 2] for p in range(ox)]
+        ends = total_of([turn_to(jnp.where(rim, own[p], 0.0), RIM * p) for p in range(ox)])
+        ends = jnp.where(here_ends, ends, pltpu.roll(turn_to(ends, RIM * ox), 4, 0))
+        tile = jnp.where(row8 < qy, tile, ends)
         s[0] = tile
         for k in range(ox // 2):
             s[1 + k] = jnp.where(lane8 < half, own[2 * k], pltpu.roll(own[2 * k + 1], half, 1))
         s[4] = tile
-        s[5] = total_of([turn_to(jnp.where(rim, own[p], 0.0), RIM * p) for p in range(ox)])
 
     def middle(s, r, width):
         depth = RIM // 2 if width > 2 else 1
@@ -351,7 +363,8 @@
         planes = []
         for dx in (-1, 0, 1):
             tiles = range(ox // 2 - depth, ox // 2) if dx < 0 else range(depth) if dx > 0 else range(ox // 2)
-            ends = rows([jnp.where(lane8 < RIM * ox + RIM, get(dx, dy, 1, 5), get(dx, dy, -1, 5)) for dy in (-1, 0, 1)])
+            ends = [jnp.where(lane8 < 2 * RIM * ox + RIM, get(dx, dy, 1, 4), get(dx, dy, -1, 4)) for dy in (-1, 0, 1)]
+            ends = [jnp.where(row8 < 4, pltpu.roll(ends[k], 4, 0), turn_to(ends[k + 1], -RIM * ox)) for k in range(2)]
             for k in tiles:
                 pair = rows([get(dx, dy, 0, 1 + k) for dy in (-1, 0, 1)])
                 for odd in (0, 1):
@@ -402,17 +415,13 @@
 
     for copy in copies:
         copy.wait()
-    g = [g_ref[i] for i in range(bx)]
-    c = [c_ref[i] for i in range(bx)]
+    g, c = ([gc0[n, WIDTH + i, EDGE:EDGE + by, :] for i in range(bx)] for n in range(2))
     for i in range(bx):
-        gc0[0, WIDTH + i, EDGE:EDGE + by, :] = g[i]
-        gc0[1, WIDTH + i, EDGE:EDGE + by, :] = c[i]
+        g_ref[i] = g[i]
     (g_last, g_first), pk[0] = pack(g)
     (c_last, c_first), pk[1] = pack(c)
     pkx[0] = g_last + turn_to(c_last, -SPAN * WIDTH)
     pkx[1] = g_first + turn_to(c_first, SPAN * WIDTH)
-    pl.semaphore_wait(barrier, greeted)
-    begin(fine_copy, close)
 
     for m in range(ox):
         xr0[m * ey + EDGE:m * ey + EDGE + by, :] = c[2 * m] + c[2 * m + 1]
@@ -420,11 +429,26 @@
     own1 = xr0[pl.ds(0, n, stride=2), :] + xr0[pl.ds(1, n, stride=2), :]
     own1 = dot(own1, down_a).reshape(ox, my, bz)
     post(s0, own1, coarsened(own1))
-    make_c = lambda o: coarse_copy(2, o, s0, r0, RIM // 2)
+
+    def relay_copy(offset):
+        dx, dy, dz = offset
+        if (dy, dz) == (0, 0):
+            return coarse_copy(2, offset, s0, r0, RIM // 2)
+        far = abs(dx) > 1 or abs(dy) > 1
+        at, size = part((-dx, 0, 0), RIM // 2)
+        if far or dz != 0:
+            at, size = 4 if dx == -1 else 0, 1
+        src = s0.at[pl.ds(at, size)] if dx == 0 else r0.at[kx + dx, ky, 1, pl.ds(at, size)]
+        goes = 0 if far else 4 if dz != 0 else at
+        return src, r0.at[kx + dx, ky - dy, 1 - dz, pl.ds(goes, size)], 5, (0, dy, dz)
+
+    along_x = [o for o in near if o[1] == o[2] == 0]
+    onwards = [o for o in near if o not in along_x]
     make_b = lambda o: coarse_copy(3, o, s1, r1, RIM // 2)
     make_d = lambda o: coarse_copy(4, o, s2, r2, 1)
-    begin(outer_copy, sides)
-    begin(make_c, near)
+    pl.semaphore_wait(barrier, greeted)
+    begin(relay_copy, along_x)
+    begin(fine_copy, close)
 
     in_y = within(row - EDGE, 1, by)
     in_z = band & within(jnp.where(lane < half, lane + bz, lane - bz), 2, bz)
@@ -444,6 +468,9 @@
         d0[i] = jnp.where(in_y & in_x, relaxation / (26.0 + gc0[1, i]), 0.0)
         d1[i] = jnp.where(in_y & in_x & in_z, relaxation / (26.0 + t1[1, i]), 0.0)
 
+    arrive(2, relay_copy, along_x)
+    begin(relay_copy, onwards)
+    begin(outer_copy, sides)
     arrive(0, fine_copy, close)
     merged = [jnp.where(low, zr[0, f], zr[1, f]) for f in range(2)]
     ends = [jnp.where(low, zrx[0, e], zrx[1, e]) for e in range(2)]
@@ -465,7 +492,7 @@
         arrive(1, outer_copy, sides)
         for i in list(range(skip)) + list(range(ex - skip, ex)):
             spread(i)
-        arrive(2, make_c, near)
+        arrive(5, relay_copy, onwards)
         c1 = middle(s0, r0, RIM)
         ok = inside1(c1.shape, RIM)
         c1 = jnp.where(ok, c1, 0.0)
@@ -602,7 +629,7 @@
     gs = jnp.sum(jnp.where(lane8[:1] < half, total, 0.0), axis=1, keepdims=True)
     ds = jnp.sum(jnp.where(lane8[:1] < half, 0.0, total), axis=1, keepdims=True)
     alpha_ref[...] = jnp.broadcast_to(gs / ds, (1, bz)).reshape(alpha_ref.shape)
-    leave([(fine_copy, close), (outer_copy, sides), (make_c, near), (make_b, near), (make_d, later)])
+    leave([(fine_copy, close), (outer_copy, sides), (relay_copy, near), (make_b, near), (make_d, later)])
     for stage in range(len(groups)):
         some = red_r.at[pl.ds(base[stage], len(mates[stage]))]
         pltpu.make_async_copy(some, some, lssem.at[stage]).wait()
@@ -625,15 +652,14 @@
         mates = [len(partners(counts, group)) for group in stages(counts)]
         f32 = jnp.float32
         vmem = pl.BlockSpec(memory_space=pltpu.VMEM)
-        messages = [pltpu.VMEM((6, 8, bz), f32)] * 3
-        messages += [pltpu.VMEM((2 * kx + 1, 2 * ky + 1, 3, 6, 8, bz), f32)] * 3
+        messages = [pltpu.VMEM((5, 8, bz), f32)] * 3
+        messages += [pltpu.VMEM((2 * kx + 1, 2 * ky + 1, 3, 5, 8, bz), f32)] * 3
         precond, image, twice, image_twice, alpha, g = pl.pallas_call(
             functools.partial(kernel, counts, block, kx, ky),
             out_shape=[pltpu.VMEM(block, f32)] * 4 + [pltpu.VMEM((1, 1, bz), f32), pltpu.VMEM(block, f32)],
             in_specs=[pl.BlockSpec(memory_space=pltpu.HBM)] * 2,
             out_specs=[vmem] * 6,
             scratch_shapes=[
-                pltpu.VMEM(block, f32),
                 pltpu.VMEM((2, ex, ey, bz), f32),
                 pltpu.VMEM((2, ex, ey, bz), f32),
                 pltpu.VMEM((2, by, bz), f32),
@@ -657,7 +683,7 @@
                 pltpu.VMEM((16 * most, 8, bz), f32),
                 pltpu.SemaphoreType.DMA((2,)),
                 pltpu.SemaphoreType.DMA,
-                pltpu.SemaphoreType.DMA((5,)),
+                pltpu.SemaphoreType.DMA((6,)),
                 pltpu.SemaphoreType.DMA((len(mates),)),
                 pltpu.SemaphoreType.DMA((len(mates),)),
             ],

time: 25.3 us -> 24.5 us (0.968)
  Pallas kernels: 23.7 us -> 23 us
    pallas_call x1, Pallas kernels: 23.7 us -> 23 us  [shards(): pl.pallas_call(functools.partial(kernel, counts, block, kx, ky), out_shap...]
where the time goes in v4:
time: 24.5 us; the launch traced here: 24.4 us
  Pallas kernels  23 us (94%)
  other arithmetic  0.76 us (3%)
  between operations  0.64 us (3%)
    pallas_call x1, Pallas kernels, shards(): pl.pallas_call(functools.partial(kernel, counts, block, kx, ky), out_shap...  23 us
    sub x1, other arithmetic, shards(): image - alpha * image_twice  0.76 us

profile of v4, /device:TPU:0, one launch (start us, length us, event | category | flops | bytes accessed | tf_op | source)
XLA Modules:
  0.0 24.4 jit_solution(12285321856587732172)
XLA Ops:
  0.6 23.0 %relayed.1 = (f32[12,16,128]{2,1,0:T(8,128)S(1)}, f32[12,16,128]{2,1,0:T(8,128)S(1)}, f32[12,16,128]{2,1,0:T(8,128)S(1)}, f32[12,16,128]{2,1,0:T(8,128)S(1)}, f3...) custom-call(f32[12,16,128]{2,1,0:T(8,128)} %g_hbm.1, f32[12,16,128]{2,1,0:T(8,128)} %c_hbm.1), custom_call_target="tpu_custom_call" | custom-call | tf_op jit(solution)/shard_map/relayed/pallas_call | solution.py:657
  23.6 0.8 %multiply_subtract_fusion = (f32[12,16,128]{2,1,0:T(8,128)}, f32[12,16,128]{2,1,0:T(8,128)}, f32[12,16,128]{2,1,0:T(8,128)}, f32[12,16,128]{2,1,0:T(8,128)}) fusion(f32[12,16,128]{2,1,0:T(8,128)S(1)} %get-tuple-element.13, f32[12,16,128]{2,1,0:T(8,128)S(1)} %get-tuple-element.15, f32[128]{0:T(128)S(1)} %bitcast.1, f32[12,16,128]{2,1,0:T(8,128)S(1)} %get-tuple-element.12, ...), kind=kLoop, calls=%fused_computation | loop fusion | flops 172032 | bytes 885248 | tf_op jit(solution)/shard_map/sub | solution.py:694

commit v5 on v4

--- a/solution.py
+++ b/solution.py
@@ -21,12 +21,10 @@
 PART = SWEEPS + 1
 
 
-def dot(a, b):
-    high = a.astype(jnp.bfloat16)
-    low = (a - high.astype(jnp.float32)).astype(jnp.bfloat16)
-    both = jnp.concatenate([high, low], 1)
-    b = b.astype(jnp.bfloat16)
-    return jnp.dot(both, jnp.concatenate([b, b], 0), preferred_element_type=jnp.float32)
+def pick(values, lanes):
+    flat = values.reshape(-1, values.shape[-1])
+    lanes = jnp.broadcast_to(lanes[:1], flat.shape)
+    return jnp.take_along_axis(flat, lanes, axis=1).reshape(values.shape)
 
 
 def iota(shape, dim):
@@ -53,7 +51,7 @@
 
 
 def kernel(counts, block, kx, ky, g_hbm, c_hbm, pre_ref, img_ref, twice_ref, image_twice_ref, alpha_ref, g_ref,
-           gc0, im0, pk, pkx, zr, zrx, t1, d0, d1, xr0, xr1, pf0, pf1, xm, um,
+           gc0, im0, pk, pkx, zr, zrx, t1, d, k27, w27, ys, xr0, xr1, pf0, pf1, xm, um,
            s0, s1, s2, r0, r1, r2, kept, mid, red_s, red_r, units, insem, ssem, rsem, lssem, lrsem):
     bx, by, bz = block
     me = [lax.axis_index(a) for a in AXES]
@@ -135,6 +133,9 @@
                 for ref in refs:
                     clear(ref)
 
+    for at in (0, EDGE + ey):
+        ys[:, :, at:at + EDGE, :] = jnp.zeros((2, ex, EDGE, bz), jnp.float32)
+
     def row_ends(dy):
         if dy == 0:
             return 0, by, EDGE
@@ -281,14 +282,38 @@
         ends = (total_of(pieces[bx - WIDTH:]), total_of(pieces[:WIDTH]))
         return ends, total_of(pieces[WIDTH:bx - WIDTH] + list(ends))
 
-    def yz(a, b):
-        sa = a + jnp.where(first, pltpu.roll(b, 1, 1), pltpu.roll(a, 1, 1))
-        sb = b + jnp.where(first, pltpu.roll(a, 1, 1), pltpu.roll(b, 1, 1))
-        sa = sa + jnp.where(last, pltpu.roll(b, bz - 1, 1), pltpu.roll(a, bz - 1, 1))
-        sb = sb + jnp.where(last, pltpu.roll(a, bz - 1, 1), pltpu.roll(b, bz - 1, 1))
-        sa = sa + pltpu.roll(sa, 1, 0) + pltpu.roll(sa, ey - 1, 0)
-        sb = sb + pltpu.roll(sb, 1, 0) + pltpu.roll(sb, ey - 1, 0)
-        return sa, sb
+    def lines(v, wide):
+        a, b = v
+        la, ra = pltpu.roll(a, 1, 1), pltpu.roll(a, bz - 1, 1)
+        lb, rb = pltpu.roll(b, 1, 1), pltpu.roll(b, bz - 1, 1)
+        sa = a + jnp.where(first, lb, la) + jnp.where(last, rb, ra)
+        return sa, b + jnp.where(first, la, lb) + jnp.where(last, ra, rb) if wide else None
+
+    def boxes(value, start, stop, wide=True):
+        held, pairs = {}, {}
+
+        def at(i):
+            if i not in held:
+                held[i] = value(i)
+            return held[i]
+
+        def pair(i):
+            if i not in pairs:
+                pairs[i] = [p + q for p, q in zip(at(i), at(i + 1))]
+            return pairs[i]
+
+        def result(i):
+            if (i - start) % 2 == 0:
+                around = [p + q for p, q in zip(at(i - 1), pair(i))]
+            else:
+                around = [p + q for p, q in zip(pair(i - 1), at(i + 1))]
+            total = []
+            for t in range(2):
+                ys[t, i, EDGE:EDGE + ey, :] = around[t]
+                total.append(around[t] + ys[t, i, EDGE - 1:EDGE - 1 + ey, :] + ys[t, i, EDGE + 1:EDGE + 1 + ey, :])
+            return lines(total, wide)
+
+        return at, result
 
     def box(v):
         s = v + pltpu.roll(v, 1, 2) + pltpu.roll(v, v.shape[2] - 1, 2)
@@ -296,13 +321,14 @@
         zero = jnp.zeros_like(s[:1])
         return s + jnp.concatenate([zero, s[:-1]], 0) + jnp.concatenate([s[1:], zero], 0)
 
-    p_, q_ = iota((bz, bz), 0), iota((bz, bz), 1)
-    down_a = jnp.where((p_ >> 1) == q_, 0.5, 0.0)
-    down_b = jnp.where(((p_ + bz) >> 1) == q_, 0.5, 0.0)
-    up_a = jnp.where((q_ >> 1) == p_, 1.0, 0.0)
-    up_b = jnp.where(((q_ + bz) >> 1) == p_, 1.0, 0.0)
-    down_c = jnp.where((p_ < half) & ((p_ >> 1) == lax.rem(q_, quarter)), 0.5, 0.0)
-    up_c = jnp.where(p_ == jnp.where(q_ < 3 * quarter, q_ >> 1, (q_ >> 1) + half), 1.0, 0.0)
+    down = (2 * lane8) % bz
+    down_c = (2 * lane8) % half
+    up_a = lane8 >> 1
+    up_b = (lane8 + bz) >> 1
+    up_c = jnp.where(lane8 < 3 * quarter, lane8 >> 1, (lane8 >> 1) + half)
+
+    def paired(v):
+        return v + pltpu.roll(v, bz - 1, v.ndim - 1)
 
     lx = ox + 2
 
@@ -315,7 +341,8 @@
         n = lx * my
         a = xr0[pl.ds(0, n, stride=2), :] + xr0[pl.ds(1, n, stride=2), :]
         b = xr1[pl.ds(0, n, stride=2), :] + xr1[pl.ds(1, n, stride=2), :]
-        return (dot(a, down_a) + dot(b, down_b)).reshape(lx, my, bz)
+        a, b = pick(paired(0.5 * a), down), pick(paired(0.5 * b), down)
+        return jnp.where(iota(a.shape, 1) < half, a, b).reshape(lx, my, bz)
 
     turn = lane8 // quarter
 
@@ -324,7 +351,7 @@
             xm[m * my:(m + 1) * my, :] = v[2 * m] + v[2 * m + 1]
         n = qx * my // 2
         a = xm[pl.ds(0, n, stride=2), :] + xm[pl.ds(1, n, stride=2), :]
-        a = dot(a, down_c)
+        a = pick(paired(0.5 * a), down_c)
         rows = my // 2
         tile = a[:rows]
         for m in range(1, qx):
@@ -427,7 +454,7 @@
         xr0[m * ey + EDGE:m * ey + EDGE + by, :] = c[2 * m] + c[2 * m + 1]
     n = ox * my
     own1 = xr0[pl.ds(0, n, stride=2), :] + xr0[pl.ds(1, n, stride=2), :]
-    own1 = dot(own1, down_a).reshape(ox, my, bz)
+    own1 = pick(paired(0.5 * own1), down).reshape(ox, my, bz)
     post(s0, own1, coarsened(own1))
 
     def relay_copy(offset):
@@ -465,8 +492,12 @@
                 piece = turn_to(merged[f], -SPAN * (i - WIDTH))
             t1[f, i] = jnp.where(band, piece, 0.0)
         in_x = within(jnp.full((ey, bz), i - WIDTH, jnp.int32), 0, bx)
-        d0[i] = jnp.where(in_y & in_x, relaxation / (26.0 + gc0[1, i]), 0.0)
-        d1[i] = jnp.where(in_y & in_x & in_z, relaxation / (26.0 + t1[1, i]), 0.0)
+        ca, cb = gc0[1, i], t1[1, i]
+        da = jnp.where(in_y & in_x, relaxation / (26.0 + ca), 0.0)
+        db = jnp.where(in_y & in_x & in_z, relaxation / (26.0 + cb), 0.0)
+        ka, kb = 27.0 + ca, 27.0 + cb
+        for ref, a, b in ((d, da, db), (k27, ka, kb), (w27, 1.0 - da * ka, 1.0 - db * kb)):
+            ref[0, i], ref[1, i] = a, b
 
     arrive(2, relay_copy, along_x)
     begin(relay_copy, onwards)
@@ -513,19 +544,15 @@
     def cycle(phase, g_at, near0, near1, s, r, make, offsets, far, width, hook, second, finish):
         def e0(i):
             a, b = g_at(i)
-            return d0[i] * a, d1[i] * b
-
-        sums = {}
+            return d[0, i] * a, d[1, i] * b
+
+        start = WIDTH - 2
+        at, result = boxes(e0, start, ex - start)
 
         def remainder(i):
-            for k in (i - 1, i, i + 1):
-                if k not in sums:
-                    sums[k] = yz(*e0(k))
             a, b = g_at(i)
-            ea, eb = e0(i)
-            ra = a - (27.0 + gc0[1, i]) * ea + sums[i - 1][0] + sums[i][0] + sums[i + 1][0]
-            rb = b - (27.0 + t1[1, i]) * eb + sums[i - 1][1] + sums[i][1] + sums[i + 1][1]
-            return ra, rb
+            sa, sb = result(i)
+            return w27[0, i] * a + sa, w27[1, i] * b + sb
 
         g1 = restricted(remainder)
         f = near0 * g1
@@ -544,7 +571,7 @@
         zero = jnp.zeros_like(e[:1])
         e = jnp.concatenate([e[xs.index(x)][None] if x in xs else zero for x in range(-reach, qx + reach)], 0)
         e = pltpu.roll(e, my - 2, 1)[:, :my // 2].reshape(nq * my // 2, bz)
-        u = dot(e, up_c)
+        u = pick(e, up_c)
         um[pl.ds(0, nq * my // 2, stride=2), :] = u
         um[pl.ds(1, nq * my // 2, stride=2), :] = u
         u = um[:nq * my, :].reshape(nq, my, bz)
@@ -559,7 +586,7 @@
         nm = mx - 2
         f = f[1:mx - 1].reshape(nm * my, bz)
         for pf, up in ((pf0, up_a), (pf1, up_b)):
-            w = dot(f, up)
+            w = pick(f, up)
             pf[pl.ds(0, nm * my, stride=2), :] = w
             pf[pl.ds(1, nm * my, stride=2), :] = w
 
@@ -568,27 +595,18 @@
             a, b = e0(i)
             return a + pf0[m * ey:(m + 1) * ey, :], b + pf1[m * ey:(m + 1) * ey, :]
 
-        sums1, sums2 = {}, {}
-        e2 = {}
         wide = width > 1
         past = INNER + 1 if wide else 1
-        for i in range(WIDTH - past, WIDTH + bx + past):
-            for k in (i - 1, i, i + 1):
-                if k not in sums1:
-                    sums1[k] = yz(*e1(k))
-            ga, gb = g_at(i)
-            ea, eb = e1(i)
-            s_ = [sums1[i - 1][t] + sums1[i][t] + sums1[i + 1][t] for t in range(2)]
-            za = ea + d0[i] * (ga - (27.0 + gc0[1, i]) * ea + s_[0])
-            zb = eb + d1[i] * (gb - (27.0 + t1[1, i]) * eb + s_[1])
-            e2[i] = za, zb
-            sums2[i] = yz(za, zb)
-            k = i - 1
-            if k - 1 in sums2:
-                around = [sums2[k - 1][t] + sums2[k][t] + sums2[k + 1][t] for t in range(2)]
-                za, zb = e2[k]
-                finish(k, za, (27.0 + gc0[1, k]) * za - around[0],
-                       (27.0 + t1[1, k]) * zb - around[1] if wide else None)
+        at1, result1 = boxes(e1, WIDTH - past, WIDTH + bx + past)
+
+        def e2(i):
+            return [w27[t, i] * a + e + d[t, i] * s_ for t, (a, e, s_) in enumerate(zip(at1(i), e0(i), result1(i)))]
+
+        at2, result2 = boxes(e2, WIDTH - past + 1, WIDTH + bx + past - 1, wide)
+        for i in range(WIDTH - past + 1, WIDTH + bx + past - 1):
+            a, b = at2(i)
+            sa, sb = result2(i)
+            finish(i, a, k27[0, i] * a - sa, k27[1, i] * b - sb if wide else None)
 
     gamma, delta = [], []
 
@@ -667,8 +685,8 @@
                 pltpu.VMEM((2, 2, ey, bz), f32),
                 pltpu.VMEM((2, 2, ey, bz), f32),
                 pltpu.VMEM((2, ex, ey, bz), f32),
-                pltpu.VMEM((ex, ey, bz), f32),
-                pltpu.VMEM((ex, ey, bz), f32),
+                *[pltpu.VMEM((2, ex, ey, bz), f32)] * 3,
+                pltpu.VMEM((2, ex, ey + 2 * EDGE, bz), f32),
                 pltpu.VMEM(((ox + 2) * ey, bz), f32),
                 pltpu.VMEM(((ox + 2) * ey, bz), f32),
                 pltpu.VMEM(((mx - 2) * ey, bz), f32),

time: 24.5 us -> 24 us (0.980)
  Pallas kernels: 23 us -> 22.5 us
    pallas_call x1, Pallas kernels: 23 us -> 22.5 us  [shards(): pl.pallas_call(functools.partial(kernel, counts, block, kx, ky), out_shap...]
where the time goes in v5:
time: 24 us; the launch traced here: 23.9 us
  Pallas kernels  22.5 us (94%)
  other arithmetic  0.76 us (3%)
  between operations  0.64 us (3%)
    pallas_call x1, Pallas kernels, shards(): pl.pallas_call(functools.partial(kernel, counts, block, kx, ky), out_shap...  22.5 us
    sub x1, other arithmetic, shards(): image - alpha * image_twice  0.76 us

profile of v5, /device:TPU:0, one launch (start us, length us, event | category | flops | bytes accessed | tf_op | source)
XLA Modules:
  0.0 23.9 jit_solution(3069758298093586763)
XLA Ops:
  0.6 22.5 %relayed.1 = (f32[12,16,128]{2,1,0:T(8,128)S(1)}, f32[12,16,128]{2,1,0:T(8,128)S(1)}, f32[12,16,128]{2,1,0:T(8,128)S(1)}, f32[12,16,128]{2,1,0:T(8,128)S(1)}, f3...) custom-call(f32[12,16,128]{2,1,0:T(8,128)} %g_hbm.1, f32[12,16,128]{2,1,0:T(8,128)} %c_hbm.1), custom_call_target="tpu_custom_call" | custom-call | tf_op jit(solution)/shard_map/relayed/pallas_call | solution.py:675
  23.1 0.8 %multiply_subtract_fusion = (f32[12,16,128]{2,1,0:T(8,128)}, f32[12,16,128]{2,1,0:T(8,128)}, f32[12,16,128]{2,1,0:T(8,128)}, f32[12,16,128]{2,1,0:T(8,128)}) fusion(f32[12,16,128]{2,1,0:T(8,128)S(1)} %get-tuple-element.13, f32[12,16,128]{2,1,0:T(8,128)S(1)} %get-tuple-element.15, f32[128]{0:T(128)S(1)} %bitcast.1, f32[12,16,128]{2,1,0:T(8,128)S(1)} %get-tuple-element.12, ...), kind=kLoop, calls=%fused_computation | loop fusion | flops 172032 | bytes 885248 | tf_op jit(solution)/shard_map/sub | solution.py:712

commit v6 on v5

--- a/solution.py
+++ b/solution.py
@@ -125,7 +125,7 @@
 
     for axis, edges in enumerate((
             [[gc0.at[:, pl.ds(0, WIDTH)], zrx.at[:, 0]], [gc0.at[:, pl.ds(WIDTH + bx, WIDTH)], zrx.at[:, 1]]],
-            [[ref.at[..., pl.ds(at, EDGE), :] for ref in (gc0, zr, zrx)] for at in (0, EDGE + by)],
+            [[ref.at[..., pl.ds(at, WIDTH), :] for ref in (gc0, zr, zrx)] for at in (EDGE - WIDTH, EDGE + by)],
             [[ref.at[side] for ref in (zr, zrx)] for side in range(2)])):
         for refs, edge in zip(edges, (0, counts[axis] - 1)):
             @pl.when(me[axis] == edge)
@@ -133,6 +133,9 @@
                 for ref in refs:
                     clear(ref)
 
+    for ref in (gc0, zr, zrx):
+        clear(ref.at[..., pl.ds(0, EDGE - WIDTH), :])
+        clear(ref.at[..., pl.ds(ey - EDGE + WIDTH, EDGE - WIDTH), :])
     for at in (0, EDGE + ey):
         ys[:, :, at:at + EDGE, :] = jnp.zeros((2, ex, EDGE, bz), jnp.float32)
 
@@ -140,8 +143,8 @@
         if dy == 0:
             return 0, by, EDGE
         if dy > 0:
-            return by - EDGE, EDGE, 0
-        return 0, EDGE, EDGE + by
+            return by - WIDTH, WIDTH, EDGE - WIDTH
+        return 0, WIDTH, EDGE + by
 
     def remote(src, dst, phase, offset):
         pltpu.make_async_remote_copy(
@@ -200,8 +203,8 @@
         size = 1
         for n in make(offset)[0].shape:
             size *= n
-        assert size % (8 * bz) == 0
-        return size // (8 * bz)
+        assert size % bz == 0
+        return size // bz
 
     def begin(make, offsets):
         for offset in offsets:
@@ -698,7 +701,7 @@
                 pltpu.VMEM((2, mx, my, bz), f32),
                 pltpu.VMEM((len(mates), 1, bz), f32),
                 pltpu.VMEM((sum(mates), 1, bz), f32),
-                pltpu.VMEM((16 * most, 8, bz), f32),
+                pltpu.VMEM((128 * most, 1, bz), f32),
                 pltpu.SemaphoreType.DMA((2,)),
                 pltpu.SemaphoreType.DMA,
                 pltpu.SemaphoreType.DMA((6,)),

time: 24 us -> 23.5 us (0.979)
  Pallas kernels: 22.5 us -> 22 us
    pallas_call x1, Pallas kernels: 22.5 us -> 22 us  [shards(): pl.pallas_call(functools.partial(kernel, counts, block, kx, ky), out_shap...]
where the time goes in v6:
time: 23.5 us; the launch traced here: 23.4 us
  Pallas kernels  22 us (94%)
  other arithmetic  0.76 us (3%)
  between operations  0.64 us (3%)
    pallas_call x1, Pallas kernels, shards(): pl.pallas_call(functools.partial(kernel, counts, block, kx, ky), out_shap...  22 us
    sub x1, other arithmetic, shards(): image - alpha * image_twice  0.76 us

profile of v6, /device:TPU:0, one launch (start us, length us, event | category | flops | bytes accessed | tf_op | source)
XLA Modules:
  0.0 23.4 jit_solution(17370559744364172367)
XLA Ops:
  0.6 22.0 %relayed.1 = (f32[12,16,128]{2,1,0:T(8,128)S(1)}, f32[12,16,128]{2,1,0:T(8,128)S(1)}, f32[12,16,128]{2,1,0:T(8,128)S(1)}, f32[12,16,128]{2,1,0:T(8,128)S(1)}, f3...) custom-call(f32[12,16,128]{2,1,0:T(8,128)} %g_hbm.1, f32[12,16,128]{2,1,0:T(8,128)} %c_hbm.1), custom_call_target="tpu_custom_call" | custom-call | tf_op jit(solution)/shard_map/relayed/pallas_call | solution.py:678
  22.6 0.8 %multiply_subtract_fusion = (f32[12,16,128]{2,1,0:T(8,128)}, f32[12,16,128]{2,1,0:T(8,128)}, f32[12,16,128]{2,1,0:T(8,128)}, f32[12,16,128]{2,1,0:T(8,128)}) fusion(f32[12,16,128]{2,1,0:T(8,128)S(1)} %get-tuple-element.13, f32[12,16,128]{2,1,0:T(8,128)S(1)} %get-tuple-element.15, f32[128]{0:T(128)S(1)} %bitcast.1, f32[12,16,128]{2,1,0:T(8,128)S(1)} %get-tuple-element.12, ...), kind=kLoop, calls=%fused_computation | loop fusion | flops 172032 | bytes 885248 | tf_op jit(solution)/shard_map/sub | solution.py:715

commit v7 on v6

--- a/solution.py
+++ b/solution.py
@@ -98,8 +98,9 @@
     copies = [pltpu.make_async_copy(src, inside0.at[n], insem.at[n]) for n, src in enumerate((g_hbm, c_hbm))]
     for copy in copies:
         copy.start()
+    greet = [o for o in near if abs(o[1]) <= 1 and (abs(o[0]) <= 1 or o[1] == o[2] == 0)]
     barrier = pltpu.get_barrier_semaphore()
-    for offset in near:
+    for offset in greet:
         @pl.when(valid(offset))
         def _(offset=offset):
             pl.semaphore_signal(barrier, inc=1, device_id=target(offset), device_id_type=MESH)
@@ -110,15 +111,13 @@
                 pl.semaphore_signal(barrier, inc=1, device_id=mate(step), device_id_type=MESH)
             greeted = greeted + len(steps)
 
-    def options(axis, far):
-        total = 1
-        for step in range(1, far + 1):
-            if counts[axis] > step:
-                total = total + (me[axis] >= step).astype(jnp.int32)
-                total = total + (me[axis] + step < counts[axis]).astype(jnp.int32)
-        return total
-
-    greeted = greeted + options(0, kx) * options(1, ky) * options(2, 1) - 1
+    def options(axis, step):
+        if counts[axis] <= step:
+            return 0
+        return (me[axis] >= step).astype(jnp.int32) + (me[axis] + step < counts[axis]).astype(jnp.int32)
+
+    around = (1 + options(0, 1)) * (1 + options(1, 1)) * (1 + options(2, 1)) - 1
+    greeted = greeted + around + sum(options(0, step) for step in range(2, kx + 1))
 
     def clear(ref):
         ref[...] = jnp.zeros(ref.shape, jnp.float32)
@@ -481,31 +480,48 @@
     begin(fine_copy, close)
 
     in_y = within(row - EDGE, 1, by)
-    in_z = band & within(jnp.where(lane < half, lane + bz, lane - bz), 2, bz)
+
+    def factors(t, i, rows, c, inverse):
+        d[t, i, rows], k27[t, i, rows] = inverse, 27.0 + c
+        w27[t, i, rows] = 1.0 - inverse * (27.0 + c)
 
     def spread(i):
-        for f in range(2):
-            if i < WIDTH:
-                k = i
-                piece = turn_to(ends[0], -SPAN * (bx - WIDTH + k - WIDTH * f))
-            elif i >= WIDTH + bx:
-                k = i - WIDTH - bx
-                piece = turn_to(ends[1], -SPAN * (k + WIDTH * f))
-            else:
-                piece = turn_to(merged[f], -SPAN * (i - WIDTH))
-            t1[f, i] = jnp.where(band, piece, 0.0)
-        in_x = within(jnp.full((ey, bz), i - WIDTH, jnp.int32), 0, bx)
-        ca, cb = gc0[1, i], t1[1, i]
-        da = jnp.where(in_y & in_x, relaxation / (26.0 + ca), 0.0)
-        db = jnp.where(in_y & in_x & in_z, relaxation / (26.0 + cb), 0.0)
-        ka, kb = 27.0 + ca, 27.0 + cb
-        for ref, a, b in ((d, da, db), (k27, ka, kb), (w27, 1.0 - da * ka, 1.0 - db * kb)):
-            ref[0, i], ref[1, i] = a, b
+        if own(i):
+            shifts = [SPAN * (i - WIDTH)] * 2
+            packs, scale = merged, 0
+        elif i < WIDTH:
+            shifts = [SPAN * (bx - WIDTH + i), SPAN * (bx - WIDTH + i - WIDTH)]
+            packs, scale = [ends[0]] * 2, 1
+        else:
+            shifts = [SPAN * (i - WIDTH - bx), SPAN * (i - bx)]
+            packs, scale = [ends[1]] * 2, 2
+        t1[0, i] = turn_to(packs[0], -shifts[0])
+        cb = t1[1, i] = turn_to(packs[1], -shifts[1])
+        factors(1, i, slice(None), cb, scales_b[scale] / (26.0 + cb))
+        for at, size in ((0, EDGE), (EDGE + by, EDGE)) if own(i) else ((0, ey),):
+            rows = slice(at, at + size)
+            c = gc0[1, i, rows]
+            factors(0, i, rows, c, scales_a[scale][rows] / (26.0 + c))
+
+    def own(i):
+        return WIDTH <= i < WIDTH + bx
+
+    def kept_if(ok):
+        return jnp.where(ok, relaxation, 0.0)
+
+    in_x = [True, me[0] > 0, me[0] + 1 < counts[0]]
+    in_z = jnp.where(lane < half, jnp.full((ey, bz), kept_if(me[2] + 1 < counts[2]), jnp.float32),
+                     jnp.full((ey, bz), kept_if(me[2] > 0), jnp.float32))
+    scales_a = [jnp.where(in_y, kept_if(ok), 0.0) for ok in in_x]
+    scales_b = [jnp.where(in_y & band & ok, in_z, 0.0) for ok in in_x]
+    for i in range(bx):
+        factors(0, WIDTH + i, slice(EDGE, EDGE + by), c[i], relaxation / (26.0 + c[i]))
 
     arrive(2, relay_copy, along_x)
-    begin(relay_copy, onwards)
+    begin(relay_copy, [o for o in onwards if abs(o[1]) <= 1])
     begin(outer_copy, sides)
     arrive(0, fine_copy, close)
+    begin(relay_copy, [o for o in onwards if abs(o[1]) > 1])
     merged = [jnp.where(low, zr[0, f], zr[1, f]) for f in range(2)]
     ends = [jnp.where(low, zrx[0, e], zrx[1, e]) for e in range(2)]
     skip = WIDTH - INNER
@@ -565,14 +581,21 @@
         arrive(phase, make, offsets)
         inv, diag = kept[0], kept[1]
         g2 = jnp.where(inv > 0.0, gathered(s, r, far), 0.0)
+        reach = (width + 1) // 2
         e = inv * g2
+        lowest = 0
         for sweep in range(SWEEPS - 1):
-            e = e + inv * (g2 - diag * e + box(e))
+            left = reach + SWEEPS - 2 - sweep
+            keep = [n for n, x in enumerate(xs) if -left <= x < qx + left]
+            some = slice(keep[0], keep[-1] + 1)
+            part_ = slice(keep[0] - lowest, keep[-1] + 1 - lowest)
+            e = e[part_] + inv[some] * (g2[some] - diag[some] * e[part_] + box(e)[part_])
+            lowest = keep[0]
         second()
-        reach = (width + 1) // 2
+        held = xs[lowest:lowest + e.shape[0]]
         nq = qx + 2 * reach
         zero = jnp.zeros_like(e[:1])
-        e = jnp.concatenate([e[xs.index(x)][None] if x in xs else zero for x in range(-reach, qx + reach)], 0)
+        e = jnp.concatenate([e[held.index(x)][None] if x in held else zero for x in range(-reach, qx + reach)], 0)
         e = pltpu.roll(e, my - 2, 1)[:, :my // 2].reshape(nq * my // 2, bz)
         u = pick(e, up_c)
         um[pl.ds(0, nq * my // 2, stride=2), :] = u
@@ -612,9 +635,6 @@
             finish(i, a, k27[0, i] * a - sa, k27[1, i] * b - sb if wide else None)
 
     gamma, delta = [], []
-
-    def own(i):
-        return WIDTH <= i < WIDTH + bx
 
     def finish1(i, e, out, out_b):
         im0[0, i] = out

time: 23.5 us -> 23.4 us (level)
  no operation moved by 1% of the time
where the time goes in v7:
time: 23.4 us; the launch traced here: 23.3 us
  Pallas kernels  21.9 us (94%)
  other arithmetic  0.76 us (3%)
  between operations  0.64 us (3%)
    pallas_call x1, Pallas kernels, shards(): pl.pallas_call(functools.partial(kernel, counts, block, kx, ky), out_shap...  21.9 us
    sub x1, other arithmetic, shards(): image - alpha * image_twice  0.76 us

profile of v7, /device:TPU:0, one launch (start us, length us, event | category | flops | bytes accessed | tf_op | source)
XLA Modules:
  0.0 23.3 jit_solution(9137615453213891822)
XLA Ops:
  0.6 21.9 %relayed.1 = (f32[12,16,128]{2,1,0:T(8,128)S(1)}, f32[12,16,128]{2,1,0:T(8,128)S(1)}, f32[12,16,128]{2,1,0:T(8,128)S(1)}, f32[12,16,128]{2,1,0:T(8,128)S(1)}, f3...) custom-call(f32[12,16,128]{2,1,0:T(8,128)} %g_hbm.1, f32[12,16,128]{2,1,0:T(8,128)} %c_hbm.1), custom_call_target="tpu_custom_call" | custom-call | tf_op jit(solution)/shard_map/relayed/pallas_call | solution.py:698
  22.5 0.8 %multiply_subtract_fusion = (f32[12,16,128]{2,1,0:T(8,128)}, f32[12,16,128]{2,1,0:T(8,128)}, f32[12,16,128]{2,1,0:T(8,128)}, f32[12,16,128]{2,1,0:T(8,128)}) fusion(f32[12,16,128]{2,1,0:T(8,128)S(1)} %get-tuple-element.13, f32[12,16,128]{2,1,0:T(8,128)S(1)} %get-tuple-element.15, f32[128]{0:T(128)S(1)} %bitcast.1, f32[12,16,128]{2,1,0:T(8,128)S(1)} %get-tuple-element.12, ...), kind=kLoop, calls=%fused_computation | loop fusion | flops 172032 | bytes 885248 | tf_op jit(solution)/shard_map/sub | solution.py:735

commit v8 on v7

--- a/solution.py
+++ b/solution.py
@@ -135,8 +135,8 @@
     for ref in (gc0, zr, zrx):
         clear(ref.at[..., pl.ds(0, EDGE - WIDTH), :])
         clear(ref.at[..., pl.ds(ey - EDGE + WIDTH, EDGE - WIDTH), :])
-    for at in (0, EDGE + ey):
-        ys[:, :, at:at + EDGE, :] = jnp.zeros((2, ex, EDGE, bz), jnp.float32)
+    for at in (0, ey):
+        ys[:, :, at:at + 2 * EDGE, :] = jnp.zeros((2, ex, 2 * EDGE, bz), jnp.float32)
 
     def row_ends(dy):
         if dy == 0:
@@ -288,10 +288,17 @@
         a, b = v
         la, ra = pltpu.roll(a, 1, 1), pltpu.roll(a, bz - 1, 1)
         lb, rb = pltpu.roll(b, 1, 1), pltpu.roll(b, bz - 1, 1)
-        sa = a + jnp.where(first, lb, la) + jnp.where(last, rb, ra)
-        return sa, b + jnp.where(first, la, lb) + jnp.where(last, ra, rb) if wide else None
-
-    def boxes(value, start, stop, wide=True):
+        f, l = first[:a.shape[0]], last[:a.shape[0]]
+        sa = a + jnp.where(f, lb, la) + jnp.where(l, rb, ra)
+        return sa, b + jnp.where(f, la, lb) + jnp.where(l, ra, rb) if wide else None
+
+    shore = WIDTH - 1
+    rows_all, rows_some = slice(0, ey), slice(EDGE - shore, EDGE + by + shore)
+
+    def moved(rows, by_):
+        return slice(rows.start + by_, rows.stop + by_)
+
+    def boxes(value, start, stop, wide=True, rows=rows_some):
         held, pairs = {}, {}
 
         def at(i):
@@ -311,8 +318,9 @@
                 around = [p + q for p, q in zip(pair(i - 1), at(i + 1))]
             total = []
             for t in range(2):
-                ys[t, i, EDGE:EDGE + ey, :] = around[t]
-                total.append(around[t] + ys[t, i, EDGE - 1:EDGE - 1 + ey, :] + ys[t, i, EDGE + 1:EDGE + 1 + ey, :])
+                ys[t, i, moved(rows, EDGE), :] = around[t]
+                mid_row = around[t] if rows is rows_some else ys[t, i, moved(rows_some, EDGE), :]
+                total.append(mid_row + ys[t, i, moved(rows_some, EDGE - 1), :] + ys[t, i, moved(rows_some, EDGE + 1), :])
             return lines(total, wide)
 
         return at, result
@@ -338,8 +346,8 @@
         for m in range(lx):
             a0, b0 = of(2 * m + INNER)
             a1, b1 = of(2 * m + INNER + 1)
-            xr0[m * ey:(m + 1) * ey, :] = a0 + a1
-            xr1[m * ey:(m + 1) * ey, :] = b0 + b1
+            xr0[moved(rows_some, m * ey), :] = a0 + a1
+            xr1[moved(rows_some, m * ey), :] = b0 + b1
         n = lx * my
         a = xr0[pl.ds(0, n, stride=2), :] + xr0[pl.ds(1, n, stride=2), :]
         b = xr1[pl.ds(0, n, stride=2), :] + xr1[pl.ds(1, n, stride=2), :]
@@ -534,7 +542,7 @@
         ok = within(iota(shape, 0) - width, 0, ox) & within(iota(shape, 1) - edge1, 1, by // 2)
         return ok & within(zl, 2, half) & (zl >= -RIM) & (zl < half + RIM)
 
-    c1 = restricted(lambda i: (gc0[1, i], t1[1, i]))
+    c1 = restricted(lambda i: (gc0[1, i, rows_some], t1[1, i, rows_some]))
     near0 = jnp.where(inside1((lx, my, bz), 1), relaxation / (26.0 + c1), 0.0)
     near1 = 27.0 + c1
 
@@ -561,17 +569,17 @@
         kept[1] = 27.0 + c2
 
     def cycle(phase, g_at, near0, near1, s, r, make, offsets, far, width, hook, second, finish):
-        def e0(i):
-            a, b = g_at(i)
-            return d[0, i] * a, d[1, i] * b
+        def e0(i, rows=rows_some):
+            a, b = g_at(i, rows)
+            return d[0, i, rows] * a, d[1, i, rows] * b
 
         start = WIDTH - 2
         at, result = boxes(e0, start, ex - start)
 
         def remainder(i):
-            a, b = g_at(i)
+            a, b = g_at(i, rows_some)
             sa, sb = result(i)
-            return w27[0, i] * a + sa, w27[1, i] * b + sb
+            return w27[0, i, rows_some] * a + sa, w27[1, i, rows_some] * b + sb
 
         g1 = restricted(remainder)
         f = near0 * g1
@@ -616,31 +624,34 @@
             pf[pl.ds(0, nm * my, stride=2), :] = w
             pf[pl.ds(1, nm * my, stride=2), :] = w
 
-        def e1(i):
+        def e1(i, rows):
             m = (i - WIDTH) // 2 + width
-            a, b = e0(i)
-            return a + pf0[m * ey:(m + 1) * ey, :], b + pf1[m * ey:(m + 1) * ey, :]
+            a, b = e0(i, rows)
+            return a + pf0[moved(rows, m * ey), :], b + pf1[moved(rows, m * ey), :]
 
         wide = width > 1
         past = INNER + 1 if wide else 1
-        at1, result1 = boxes(e1, WIDTH - past, WIDTH + bx + past)
+        rows1 = rows_all if wide else rows_some
+        at1, result1 = boxes(lambda i: e1(i, rows1), WIDTH - past, WIDTH + bx + past, rows=rows1)
 
         def e2(i):
-            return [w27[t, i] * a + e + d[t, i] * s_ for t, (a, e, s_) in enumerate(zip(at1(i), e0(i), result1(i)))]
+            values = e1(i, rows_some) if wide else at1(i)
+            return [w27[t, i, rows_some] * a + e + d[t, i, rows_some] * s_
+                    for t, (a, e, s_) in enumerate(zip(values, e0(i), result1(i)))]
 
         at2, result2 = boxes(e2, WIDTH - past + 1, WIDTH + bx + past - 1, wide)
         for i in range(WIDTH - past + 1, WIDTH + bx + past - 1):
             a, b = at2(i)
             sa, sb = result2(i)
-            finish(i, a, k27[0, i] * a - sa, k27[1, i] * b - sb if wide else None)
+            finish(i, a, k27[0, i, rows_some] * a - sa, k27[1, i, rows_some] * b - sb if wide else None)
 
     gamma, delta = [], []
 
     def finish1(i, e, out, out_b):
-        im0[0, i] = out
-        im0[1, i] = out_b
+        im0[0, i, rows_some] = out
+        im0[1, i, rows_some] = out_b
         if own(i):
-            e, out = e[EDGE:EDGE + by], out[EDGE:EDGE + by]
+            e, out = e[shore:shore + by], im0[0, i, EDGE:EDGE + by]
             pre_ref[i - WIDTH] = e
             img_ref[i - WIDTH] = out
             gamma.append(g_ref[i - WIDTH] * e)
@@ -652,18 +663,18 @@
             sum_begin(0, jnp.where(lane8[:1] < half, gs, ds))
 
     nothing = lambda: None
-    cycle(3, lambda i: (gc0[0, i], t1[0, i]), near0, near1, s1, r1, make_b, near, ky, RIM - 1, coefficients, nothing, finish1)
+    cycle(3, lambda i, rows: (gc0[0, i, rows], t1[0, i, rows]), near0, near1, s1, r1, make_b, near, ky, RIM - 1, coefficients, nothing, finish1)
 
     def relay(stage):
         if len(groups) > 1:
             sum_begin(stage, sum_end(stage - 1))
 
     def finish2(i, e, out, out_b):
-        twice_ref[i - WIDTH] = e[EDGE:EDGE + by]
-        image_twice_ref[i - WIDTH] = out[EDGE:EDGE + by]
+        twice_ref[i - WIDTH] = e[shore:shore + by]
+        image_twice_ref[i - WIDTH] = out[shore:shore + by]
 
     skip1 = RIM - 1
-    cycle(4, lambda i: (im0[0, i], im0[1, i]), mid[0, skip1:skip1 + lx], mid[1, skip1:skip1 + lx], s2, r2, make_d, later, 1, 1,
+    cycle(4, lambda i, rows: (im0[0, i, rows], im0[1, i, rows]), mid[0, skip1:skip1 + lx], mid[1, skip1:skip1 + lx], s2, r2, make_d, later, 1, 1,
           lambda: relay(1), lambda: relay(2), finish2)
 
     total = sum_end(len(groups) - 1)

time: 23.4 us -> 23.2 us (level)
  no operation moved by 1% of the time
where the time goes in v8:
time: 23.2 us; the launch traced here: 23.1 us
  Pallas kernels  21.7 us (94%)
  other arithmetic  0.76 us (3%)
  between operations  0.64 us (3%)
    pallas_call x1, Pallas kernels, shards(): pl.pallas_call(functools.partial(kernel, counts, block, kx, ky), out_shap...  21.7 us
    sub x1, other arithmetic, shards(): image - alpha * image_twice  0.76 us

profile of v8, /device:TPU:0, one launch (start us, length us, event | category | flops | bytes accessed | tf_op | source)
XLA Modules:
  0.0 23.1 jit_solution(8535107194464828427)
XLA Ops:
  0.6 21.7 %relayed.1 = (f32[12,16,128]{2,1,0:T(8,128)S(1)}, f32[12,16,128]{2,1,0:T(8,128)S(1)}, f32[12,16,128]{2,1,0:T(8,128)S(1)}, f32[12,16,128]{2,1,0:T(8,128)S(1)}, f3...) custom-call(f32[12,16,128]{2,1,0:T(8,128)} %g_hbm.1, f32[12,16,128]{2,1,0:T(8,128)} %c_hbm.1), custom_call_target="tpu_custom_call" | custom-call | tf_op jit(solution)/shard_map/relayed/pallas_call | solution.py:709
  22.3 0.8 %multiply_subtract_fusion = (f32[12,16,128]{2,1,0:T(8,128)}, f32[12,16,128]{2,1,0:T(8,128)}, f32[12,16,128]{2,1,0:T(8,128)}, f32[12,16,128]{2,1,0:T(8,128)}) fusion(f32[12,16,128]{2,1,0:T(8,128)S(1)} %get-tuple-element.13, f32[12,16,128]{2,1,0:T(8,128)S(1)} %get-tuple-element.15, f32[128]{0:T(128)S(1)} %bitcast.1, f32[12,16,128]{2,1,0:T(8,128)S(1)} %get-tuple-element.12, ...), kind=kLoop, calls=%fused_computation | loop fusion | flops 172032 | bytes 885248 | tf_op jit(solution)/shard_map/sub | solution.py:746

commit v9 on v8

--- a/solution.py
+++ b/solution.py
@@ -51,7 +51,7 @@
 
 
 def kernel(counts, block, kx, ky, g_hbm, c_hbm, pre_ref, img_ref, twice_ref, image_twice_ref, alpha_ref, g_ref,
-           gc0, im0, pk, pkx, zr, zrx, t1, d, k27, w27, ys, xr0, xr1, pf0, pf1, xm, um,
+           gc0, im0, pk, pkx, zr, zrx, t1, d, k27, w27, ys, xr0, xr1, pf0, pf1, sf0, sf1, se, xm, um,
            s0, s1, s2, r0, r1, r2, kept, mid, red_s, red_r, units, insem, ssem, rsem, lssem, lrsem):
     bx, by, bz = block
     me = [lax.axis_index(a) for a in AXES]
@@ -335,6 +335,7 @@
     down_c = (2 * lane8) % half
     up_a = lane8 >> 1
     up_b = (lane8 + bz) >> 1
+    aside = 2 * (lane8 & 1) - 1
     up_c = jnp.where(lane8 < 3 * quarter, lane8 >> 1, (lane8 >> 1) + half)
 
     def paired(v):
@@ -546,10 +547,12 @@
     near0 = jnp.where(inside1((lx, my, bz), 1), relaxation / (26.0 + c1), 0.0)
     near1 = 27.0 + c1
 
-    def coefficients():
+    def outer():
         arrive(1, outer_copy, sides)
         for i in list(range(skip)) + list(range(ex - skip, ex)):
             spread(i)
+
+    def coefficients():
         arrive(5, relay_copy, onwards)
         c1 = middle(s0, r0, RIM)
         ok = inside1(c1.shape, RIM)
@@ -579,12 +582,19 @@
         def remainder(i):
             a, b = g_at(i, rows_some)
             sa, sb = result(i)
+            if phase == 4:
+                se[0, i, rows_some], se[1, i, rows_some] = sa, sb
             return w27[0, i, rows_some] * a + sa, w27[1, i, rows_some] * b + sb
 
         g1 = restricted(remainder)
         f = near0 * g1
         post(s, g1[1:1 + ox], coarsened((g1 - near1 * f + box(f))[1:1 + ox]))
         begin(make, offsets)
+        if phase == 3:
+            outer()
+            whole = boxes(lambda i: e0(i, rows_all), 1, ex - 1, rows=rows_all)[1]
+            for i in range(1, ex - 1):
+                se[0, i, rows_some], se[1, i, rows_some] = whole(i)
         hook()
         arrive(phase, make, offsets)
         inv, diag = kept[0], kept[1]
@@ -619,8 +629,12 @@
         f = f + inv * (g1 - diag * f + box(f))
         nm = mx - 2
         f = f[1:mx - 1].reshape(nm * my, bz)
-        for pf, up in ((pf0, up_a), (pf1, up_b)):
+        for pf, sf, up in ((pf0, sf0, up_a), (pf1, sf1, up_b)):
             w = pick(f, up)
+            z = (w + w + pick(f, (up + aside) % bz)).reshape(nm, my, bz)
+            for odd in range(2):
+                y = z + z + pltpu.roll(z, my - 1 if odd else 1, 1)
+                sf[pl.ds(odd, nm * my, stride=2), :] = y.reshape(nm * my, bz)
             pf[pl.ds(0, nm * my, stride=2), :] = w
             pf[pl.ds(1, nm * my, stride=2), :] = w
 
@@ -631,11 +645,18 @@
 
         wide = width > 1
         past = INNER + 1 if wide else 1
-        rows1 = rows_all if wide else rows_some
-        at1, result1 = boxes(lambda i: e1(i, rows1), WIDTH - past, WIDTH + bx + past, rows=rows1)
+        def result1(i):
+            x = i - WIDTH
+            m = x // 2 + width
+            n = m + 1 if x % 2 else m - 1
+            total = []
+            for t, sf in enumerate((sf0, sf1)):
+                here = sf[moved(rows_some, m * ey), :]
+                total.append(se[t, i, rows_some] + (here + here + sf[moved(rows_some, n * ey), :]))
+            return total
 
         def e2(i):
-            values = e1(i, rows_some) if wide else at1(i)
+            values = e1(i, rows_some)
             return [w27[t, i, rows_some] * a + e + d[t, i, rows_some] * s_
                     for t, (a, e, s_) in enumerate(zip(values, e0(i), result1(i)))]
 
@@ -723,8 +744,8 @@
                 pltpu.VMEM((2, ex, ey + 2 * EDGE, bz), f32),
                 pltpu.VMEM(((ox + 2) * ey, bz), f32),
                 pltpu.VMEM(((ox + 2) * ey, bz), f32),
-                pltpu.VMEM(((mx - 2) * ey, bz), f32),
-                pltpu.VMEM(((mx - 2) * ey, bz), f32),
+                *[pltpu.VMEM(((mx - 2) * ey, bz), f32)] * 4,
+                pltpu.VMEM((2, ex, ey, bz), f32),
                 pltpu.VMEM((qx * my, bz), f32),
                 pltpu.VMEM(((qx + 4) * my, bz), f32),
                 *messages,

time: 23.2 us -> 22.8 us (0.983)
  Pallas kernels: 21.7 us -> 21.2 us
    pallas_call x1, Pallas kernels: 21.7 us -> 21.2 us  [shards(): pl.pallas_call(functools.partial(kernel, counts, block, kx, ky), out_shap...]
where the time goes in v9:
time: 22.8 us; the launch traced here: 22.6 us
  Pallas kernels  21.2 us (93%)
  other arithmetic  0.76 us (3%)
  between operations  0.64 us (3%)
    pallas_call x1, Pallas kernels, shards(): pl.pallas_call(functools.partial(kernel, counts, block, kx, ky), out_shap...  21.2 us
    sub x1, other arithmetic, shards(): image - alpha * image_twice  0.76 us

profile of v9, /device:TPU:0, one launch (start us, length us, event | category | flops | bytes accessed | tf_op | source)
XLA Modules:
  0.0 22.6 jit_solution(8445921769347141083)
XLA Ops:
  0.6 21.2 %relayed.1 = (f32[12,16,128]{2,1,0:T(8,128)S(1)}, f32[12,16,128]{2,1,0:T(8,128)S(1)}, f32[12,16,128]{2,1,0:T(8,128)S(1)}, f32[12,16,128]{2,1,0:T(8,128)S(1)}, f3...) custom-call(f32[12,16,128]{2,1,0:T(8,128)} %g_hbm.1, f32[12,16,128]{2,1,0:T(8,128)} %c_hbm.1), custom_call_target="tpu_custom_call" | custom-call | tf_op jit(solution)/shard_map/relayed/pallas_call | solution.py:730
  21.9 0.8 %multiply_subtract_fusion = (f32[12,16,128]{2,1,0:T(8,128)}, f32[12,16,128]{2,1,0:T(8,128)}, f32[12,16,128]{2,1,0:T(8,128)}, f32[12,16,128]{2,1,0:T(8,128)}) fusion(f32[12,16,128]{2,1,0:T(8,128)S(1)} %get-tuple-element.13, f32[12,16,128]{2,1,0:T(8,128)S(1)} %get-tuple-element.15, f32[128]{0:T(128)S(1)} %bitcast.1, f32[12,16,128]{2,1,0:T(8,128)S(1)} %get-tuple-element.12, ...), kind=kLoop, calls=%fused_computation | loop fusion | flops 172032 | bytes 885248 | tf_op jit(solution)/shard_map/sub | solution.py:767

commit v10 on v9

--- a/solution.py
+++ b/solution.py
@@ -485,8 +485,9 @@
     make_b = lambda o: coarse_copy(3, o, s1, r1, RIM // 2)
     make_d = lambda o: coarse_copy(4, o, s2, r2, 1)
     pl.semaphore_wait(barrier, greeted)
+    begin(fine_copy, [o for o in close if sum(map(abs, o)) > 1])
     begin(relay_copy, along_x)
-    begin(fine_copy, close)
+    begin(fine_copy, [o for o in close if sum(map(abs, o)) == 1])
 
     in_y = within(row - EDGE, 1, by)
 
@@ -576,6 +577,10 @@
             a, b = g_at(i, rows)
             return d[0, i, rows] * a, d[1, i, rows] * b
 
+        def settle(i, sums):
+            for t, (e, s_) in enumerate(zip(e0(i), sums)):
+                se[t, i, rows_some] = (w27[t, i, rows_some] + 1.0) * e + d[t, i, rows_some] * s_
+
         start = WIDTH - 2
         at, result = boxes(e0, start, ex - start)
 
@@ -594,7 +599,10 @@
             outer()
             whole = boxes(lambda i: e0(i, rows_all), 1, ex - 1, rows=rows_all)[1]
             for i in range(1, ex - 1):
-                se[0, i, rows_some], se[1, i, rows_some] = whole(i)
+                settle(i, whole(i))
+        else:
+            for i in range(WIDTH - 1, WIDTH + bx + 1):
+                settle(i, [se[t, i, rows_some] for t in range(2)])
         hook()
         arrive(phase, make, offsets)
         inv, diag = kept[0], kept[1]
@@ -638,27 +646,19 @@
             pf[pl.ds(0, nm * my, stride=2), :] = w
             pf[pl.ds(1, nm * my, stride=2), :] = w
 
-        def e1(i, rows):
-            m = (i - WIDTH) // 2 + width
-            a, b = e0(i, rows)
-            return a + pf0[moved(rows, m * ey), :], b + pf1[moved(rows, m * ey), :]
-
         wide = width > 1
         past = INNER + 1 if wide else 1
-        def result1(i):
+        def e2(i):
             x = i - WIDTH
             m = x // 2 + width
             n = m + 1 if x % 2 else m - 1
-            total = []
-            for t, sf in enumerate((sf0, sf1)):
+            values = []
+            for t, (pf, sf) in enumerate(((pf0, sf0), (pf1, sf1))):
                 here = sf[moved(rows_some, m * ey), :]
-                total.append(se[t, i, rows_some] + (here + here + sf[moved(rows_some, n * ey), :]))
-            return total
-
-        def e2(i):
-            values = e1(i, rows_some)
-            return [w27[t, i, rows_some] * a + e + d[t, i, rows_some] * s_
-                    for t, (a, e, s_) in enumerate(zip(values, e0(i), result1(i)))]
+                around = here + here + sf[moved(rows_some, n * ey), :]
+                values.append(se[t, i, rows_some] + w27[t, i, rows_some] * pf[moved(rows_some, m * ey), :]
+                              + d[t, i, rows_some] * around)
+            return values
 
         at2, result2 = boxes(e2, WIDTH - past + 1, WIDTH + bx + past - 1, wide)
         for i in range(WIDTH - past + 1, WIDTH + bx + past - 1):

time: 22.8 us -> 22.5 us (0.987)
  no operation moved by 1% of the time
where the time goes in v10:
time: 22.5 us; the launch traced here: 22.4 us
  Pallas kernels  21 us (93%)
  other arithmetic  0.76 us (3%)
  between operations  0.64 us (3%)
    pallas_call x1, Pallas kernels, shards(): pl.pallas_call(functools.partial(kernel, counts, block, kx, ky), out_shap...  21 us
    sub x1, other arithmetic, shards(): image - alpha * image_twice  0.76 us

profile of v10, /device:TPU:0, one launch (start us, length us, event | category | flops | bytes accessed | tf_op | source)
XLA Modules:
  0.0 22.4 jit_solution(16768464430848400729)
XLA Ops:
  0.6 21.0 %relayed.1 = (f32[12,16,128]{2,1,0:T(8,128)S(1)}, f32[12,16,128]{2,1,0:T(8,128)S(1)}, f32[12,16,128]{2,1,0:T(8,128)S(1)}, f32[12,16,128]{2,1,0:T(8,128)S(1)}, f3...) custom-call(f32[12,16,128]{2,1,0:T(8,128)} %g_hbm.1, f32[12,16,128]{2,1,0:T(8,128)} %c_hbm.1), custom_call_target="tpu_custom_call" | custom-call | tf_op jit(solution)/shard_map/relayed/pallas_call | solution.py:730
  21.6 0.8 %multiply_subtract_fusion = (f32[12,16,128]{2,1,0:T(8,128)}, f32[12,16,128]{2,1,0:T(8,128)}, f32[12,16,128]{2,1,0:T(8,128)}, f32[12,16,128]{2,1,0:T(8,128)}) fusion(f32[12,16,128]{2,1,0:T(8,128)S(1)} %get-tuple-element.13, f32[12,16,128]{2,1,0:T(8,128)S(1)} %get-tuple-element.15, f32[128]{0:T(128)S(1)} %bitcast.1, f32[12,16,128]{2,1,0:T(8,128)S(1)} %get-tuple-element.12, ...), kind=kLoop, calls=%fused_computation | loop fusion | flops 172032 | bytes 885248 | tf_op jit(solution)/shard_map/sub | solution.py:767

commit v11 on v10

--- a/solution.py
+++ b/solution.py
@@ -529,9 +529,9 @@
 
     arrive(2, relay_copy, along_x)
     begin(relay_copy, [o for o in onwards if abs(o[1]) <= 1])
-    begin(outer_copy, sides)
     arrive(0, fine_copy, close)
     begin(relay_copy, [o for o in onwards if abs(o[1]) > 1])
+    begin(outer_copy, sides)
     merged = [jnp.where(low, zr[0, f], zr[1, f]) for f in range(2)]
     ends = [jnp.where(low, zrx[0, e], zrx[1, e]) for e in range(2)]
     skip = WIDTH - INNER

time: 22.5 us -> 22.3 us (level)
  Pallas kernels: 21 us -> 20.7 us
    pallas_call x1, Pallas kernels: 21 us -> 20.7 us  [shards(): pl.pallas_call(functools.partial(kernel, counts, block, kx, ky), out_shap...]
where the time goes in v11:
time: 22.3 us; the launch traced here: 22.1 us
  Pallas kernels  20.7 us (93%)
  other arithmetic  0.76 us (3%)
  between operations  0.64 us (3%)
    pallas_call x1, Pallas kernels, shards(): pl.pallas_call(functools.partial(kernel, counts, block, kx, ky), out_shap...  20.7 us
    sub x1, other arithmetic, shards(): image - alpha * image_twice  0.76 us

profile of v11, /device:TPU:0, one launch (start us, length us, event | category | flops | bytes accessed | tf_op | source)
XLA Modules:
  0.0 22.1 jit_solution(12571998738588479659)
XLA Ops:
  0.6 20.7 %relayed.1 = (f32[12,16,128]{2,1,0:T(8,128)S(1)}, f32[12,16,128]{2,1,0:T(8,128)S(1)}, f32[12,16,128]{2,1,0:T(8,128)S(1)}, f32[12,16,128]{2,1,0:T(8,128)S(1)}, f3...) custom-call(f32[12,16,128]{2,1,0:T(8,128)} %g_hbm.1, f32[12,16,128]{2,1,0:T(8,128)} %c_hbm.1), custom_call_target="tpu_custom_call" | custom-call | tf_op jit(solution)/shard_map/relayed/pallas_call | solution.py:730
  21.4 0.8 %multiply_subtract_fusion = (f32[12,16,128]{2,1,0:T(8,128)}, f32[12,16,128]{2,1,0:T(8,128)}, f32[12,16,128]{2,1,0:T(8,128)}, f32[12,16,128]{2,1,0:T(8,128)}) fusion(f32[12,16,128]{2,1,0:T(8,128)S(1)} %get-tuple-element.13, f32[12,16,128]{2,1,0:T(8,128)S(1)} %get-tuple-element.15, f32[128]{0:T(128)S(1)} %bitcast.1, f32[12,16,128]{2,1,0:T(8,128)S(1)} %get-tuple-element.12, ...), kind=kLoop, calls=%fused_computation | loop fusion | flops 172032 | bytes 885248 | tf_op jit(solution)/shard_map/sub | solution.py:767
